TPU v7x, 128 devices: a whole 4x4x4 slice. The times are simulated.
128 devices in a mesh: head: 8 (over z_lo, x), blk: 16 (over z_hi, y, core).
Axes of the slice: x: 4, y: 4, z: 4 (z_hi: 2, z_lo: 2; z = z_hi * 2 + z_lo), core: 2. Of those that a mesh axis runs over, the one named last changes fastest.
Arguments:
- hidden_in: bfloat16 [8192, 4096], P(('blk', 'head')), may hold values from -6 to 6
- queries: bfloat16 [8192, 2048], P(('blk', 'head')), may hold values from -26 to 26
- key_states: bfloat16 [8192, 1024], P(('blk', 'head')), may hold values from -5 to 5
- value_states: bfloat16 [8192, 1024], P(('blk', 'head')), may hold values from -6 to 6
- out_weight: bfloat16 [2048, 4096], P('head'), may hold values from -0.125 to 0.125
- norm_gain: float32 [4096], replicated, may hold values from 0.1 to 1.9
- gate_weight: bfloat16 [4096, 7168], P(None, 'head'), may hold values from -0.09375 to 0.09375
- up_weight: bfloat16 [4096, 7168], P(None, 'head'), may hold values from -0.09375 to 0.09375
- down_weight: bfloat16 [7168, 4096], P('head'), may hold values from -0.0625 to 0.0625
Outputs:
- layer_out: bfloat16 [8192, 4096], P(('blk', 'head'))
All inputs are finite; a program needn't handle non-finite values.
Results may differ from a plain program's by a relative error of at most 0.018.
Values may be sent and summed in bfloat16 or wider, within the bound.
No kernel may reach another device: no remote copies, remote signals or barrier semaphores. Data moves between devices by JAX's collectives and lax.ppermute only.
A program may use at most 192 MiB of HBM per device.

v0:
```python
import functools

import jax
import jax.numpy as jnp
from jax import lax
from jax.experimental import pallas as pl
from jax.experimental.pallas import tpu as pltpu
from jax.sharding import PartitionSpec as P


HEAD_DIM = 128
BF = jnp.bfloat16
F32 = jnp.float32
NEG = -1e30
SCALE2 = HEAD_DIM**-0.5 * 1.4426950408889634
VLIM = 56 * 1024 * 1024


def flat(x, y, z, c):
    return ((z % 2) * 4 + x) * 16 + (z // 2) * 8 + y * 2 + c


def move(a, f):
    pairs = []
    for x in range(4):
        for y in range(4):
            for z in range(4):
                for c in range(2):
                    tx, ty, tz, tc = f(x, y, z, c)
                    pairs.append((flat(x, y, z, c), flat(tx % 4, ty % 4, tz % 4, tc)))
    return lax.ppermute(a, ("head", "blk"), pairs)


def x_by(d):
    return lambda x, y, z, c: (x + d, y, z, c)


def x_out(x, y, z, c):
    return (x + 1 if c == 0 else x - 1, y, z, c)


def core_swap(x, y, z, c):
    return (x, y, z, 1 - c)


def z_low_pair(x, y, z, c):
    return (x, y, z ^ 1, c)


def z_pair(x, y, z, c):
    return (x, y, z ^ 1 if c == 0 else 3 - z, c)


def blk_by(dy, dz):
    return lambda x, y, z, c: (x, y + dy, z + 2 * dz, c)


ROWS = 256


def flash_body(q2, k, va, m_ref, acc_ref, qi, mask):
    for h in range(2):
        for r in range(512 // ROWS):
            rows = pl.ds(r * ROWS, ROWS)
            q = q2[qi, rows, h * 128 : (h + 1) * 128]
            s = lax.dot_general(q, k, (((1,), (1,)), ((), ())), preferred_element_type=F32)
            if mask:
                ri = lax.broadcasted_iota(jnp.int32, s.shape, 0) + r * ROWS
                ci = lax.broadcasted_iota(jnp.int32, s.shape, 1)
                s = jnp.where(ci <= ri, s, NEG)
            m_old = m_ref[qi, h, rows, :]
            m_new = jnp.maximum(m_old, jnp.max(s, axis=-1, keepdims=True) * SCALE2)
            p = jnp.exp2(s * SCALE2 - m_new[:, :1]).astype(BF)
            alpha = jnp.exp2(m_old - m_new)
            pv = jnp.dot(p, va, preferred_element_type=F32)
            acc = acc_ref[qi, h, rows, :]
            acc_ref[qi, h, rows, :] = acc * jnp.concatenate([alpha, alpha], axis=1) + pv
            m_ref[qi, h, rows, :] = m_new


def flash_kernel(n, first, ids, q_own, q_oth, *refs):
    kvs, refs = refs[:n], refs[n:]
    if not first:
        init, refs = refs[:4], refs[4:]
    outs, (q2, kk, va, m_ref, acc_ref) = refs[:4], refs[4:]
    q2[0] = q_own[...]
    q2[1] = q_oth[...]
    for j in range(n):
        kk[j] = kvs[j][:, :128]
        va[j, :, :128] = kvs[j][:, 128:]
        va[j, :, 128:] = jnp.ones((512, 128), BF)
    if first:
        m_ref[...] = jnp.full(m_ref.shape, NEG, F32)
        acc_ref[...] = jnp.zeros(acc_ref.shape, F32)
        flash_body(q2, kk[0], va[0], m_ref, acc_ref, 0, True)
    else:
        for qi in range(2):
            for h in range(2):
                lse = jnp.broadcast_to(init[2 * qi + 1][:, h : h + 1], (512, 128))
                m_ref[qi, h] = lse
                acc_ref[qi, h, :, :128] = init[2 * qi][:, h * 128 : (h + 1) * 128]
                acc_ref[qi, h, :, 128:] = jnp.where(lse > NEG, 1.0, 0.0)

    lead = 1 if first else 0

    def step(t, carry):
        qi = (t >= n - lead).astype(jnp.int32)
        j = t - qi * (n - lead) + lead * (1 - qi)

        @pl.when(ids[j] < ids[n + qi])
        def _():
            flash_body(q2, kk[j], va[j], m_ref, acc_ref, qi, False)

        return carry

    lax.fori_loop(0, 2 * n - lead, step, 0)
    lane = lax.broadcasted_iota(jnp.int32, (512, 128), 1)
    for qi in range(2):
        o_ref, ml = outs[2 * qi], outs[2 * qi + 1]
        lse = []
        for h in range(2):
            total = acc_ref[qi, h, :, 128:]
            seen = total > 0.0
            safe = jnp.where(seen, total, 1.0)
            o_ref[:, h * 128 : (h + 1) * 128] = (acc_ref[qi, h, :, :128] / safe).astype(o_ref.dtype)
            lse.append(jnp.where(seen, m_ref[qi, h] + jnp.log2(safe), NEG))
        ml[...] = jnp.where(lane == 0, lse[0], lse[1])


def flash(ids, q_own, q_oth, kvs, init=None, last=True):
    vm = pl.BlockSpec(memory_space=pltpu.VMEM)
    n = len(kvs)
    extra = [] if init is None else list(init)
    oth = BF if last else F32
    return pl.pallas_call(
        functools.partial(flash_kernel, n, init is None),
        in_specs=[pl.BlockSpec(memory_space=pltpu.SMEM)] + [vm] * (2 + n + len(extra)),
        out_specs=[vm] * 4,
        out_shape=[
            jax.ShapeDtypeStruct((512, 256), F32),
            jax.ShapeDtypeStruct((512, 128), F32),
            jax.ShapeDtypeStruct((512, 256), oth),
            jax.ShapeDtypeStruct((512, 128), F32),
        ],
        scratch_shapes=[
            pltpu.VMEM((2, 512, 256), BF),
            pltpu.VMEM((n, 512, 128), BF),
            pltpu.VMEM((n, 512, 256), BF),
            pltpu.VMEM((2, 2, 512, 128), F32),
            pltpu.VMEM((2, 2, 512, 256), F32),
        ],
        compiler_params=pltpu.CompilerParams(vmem_limit_bytes=VLIM),
        cost_estimate=pl.CostEstimate(flops=1_100_000_000 * n, transcendentals=0, bytes_accessed=4 << 20),
    )(ids, q_own, q_oth, *kvs, *extra)


def merge_kernel(o_own, ml_own, o_in, ml_in, out):
    for h in range(2):
        a = ml_own[:, h : h + 1]
        b = ml_in[:, h : h + 1]
        top = jnp.maximum(a, b)
        wa = jnp.exp2(a - top)
        wb = jnp.exp2(b - top)
        tot = wa + wb
        cols = slice(h * 128, (h + 1) * 128)
        res = o_own[:, cols] * (wa / tot) + o_in[:, cols].astype(F32) * (wb / tot)
        res = res.astype(BF)
        for zl in range(2):
            for x in range(4):
                lo = (zl * 4 + x) * 64
                out[x, zl, :, cols] = res[lo : lo + 64]


def merge(*args):
    vm = pl.BlockSpec(memory_space=pltpu.VMEM)
    return pl.pallas_call(
        merge_kernel,
        in_specs=[vm] * 4,
        out_specs=vm,
        out_shape=jax.ShapeDtypeStruct((4, 2, 64, 256), BF),
        cost_estimate=pl.CostEstimate(flops=1_000_000, transcendentals=0, bytes_accessed=1 << 20),
        name="merge",
    )(*args)


def proj_kernel(ids, att, own_w, *refs):
    ws, (own, oth, wbuf, sems) = refs[:6], refs[6:]
    zl, c = ids[4], ids[5]
    near, far = pl.multiple_of(c * 128, 128), pl.multiple_of((1 - c) * 128, 128)
    lo, hi = pl.ds(near, 128), pl.ds(far, 128)
    copies = [(own_w.at[pl.ds(0, 128)], 0, pl.ds(0, 128)), (own_w.at[pl.ds(128, 128)], 0, pl.ds(128, 128))]
    copies += [(w, p, d) for w, p, d in zip(ws, (1, 1, 2, 2, 3, 3), (lo, hi, lo, hi, lo, hi))]
    dmas = [pltpu.make_async_copy(src, wbuf.at[p, d], sems.at[i]) for i, (src, p, d) in enumerate(copies)]
    for d in dmas[:PDEPTH]:
        d.start()
    for p in range(4):
        for i in (2 * p, 2 * p + 1):
            dmas[i].wait()
            if i + PDEPTH < 8:
                dmas[i + PDEPTH].start()
        xs = ids[p]
        a = jnp.concatenate([att[xs, zl], att[xs, 1 - zl]], axis=0)
        for n in range(4):
            cols = slice(n * 1024, (n + 1) * 1024)
            part = jnp.dot(a, wbuf[p, :, cols], preferred_element_type=F32)
            if p == 0:
                own[:, cols] = part[:64]
            else:
                own[:, cols] += part[:64]
            if p == 0:
                oth[:, cols] = part[64:]
            else:
                oth[:, cols] += part[64:]


def proj_outer(ids, att, own_w, *refs):
    ws, (own, oth, wbuf, acc, sems) = refs[:6], refs[6:]
    proj_kernel(ids, att, own_w, *ws, own, acc, wbuf, sems)
    oth[...] = acc[...].astype(BF)


def project(ids, att, own_w, ws):
    vm = pl.BlockSpec(memory_space=pltpu.VMEM)
    hb = pl.BlockSpec(memory_space=pltpu.HBM)
    return pl.pallas_call(
        proj_outer,
        in_specs=[pl.BlockSpec(memory_space=pltpu.SMEM), vm] + [hb] * 7,
        out_specs=[vm] * 2,
        out_shape=[jax.ShapeDtypeStruct((64, 4096), F32), jax.ShapeDtypeStruct((64, 4096), BF)],
        scratch_shapes=[
            pltpu.VMEM((4, 256, 4096), BF),
            pltpu.VMEM((64, 4096), F32),
            pltpu.SemaphoreType.DMA((8,)),
        ],
        compiler_params=pltpu.CompilerParams(vmem_limit_bytes=VLIM),
        cost_estimate=pl.CostEstimate(flops=1_100_000_000, transcendentals=0, bytes_accessed=9 << 20),
        name="project",
    )(ids, att, own_w, *ws)


def norm_kernel(hid, own, got, gain, res_out, nrm_out):
    res = (hid[...].astype(F32) + (own[...] + got[...].astype(F32))).astype(BF)
    res_out[...] = res
    wide = res.astype(F32)
    ms = jnp.mean(wide * wide, axis=-1, keepdims=True)
    nrm_out[...] = (wide * lax.rsqrt(ms + 1e-05) * gain[...]).astype(BF)


def residual_norm(hid, own, got, gain):
    vm = pl.BlockSpec(memory_space=pltpu.VMEM)
    return pl.pallas_call(
        norm_kernel,
        in_specs=[vm] * 4,
        out_specs=[vm] * 2,
        out_shape=[jax.ShapeDtypeStruct((64, 4096), BF)] * 2,
        cost_estimate=pl.CostEstimate(flops=2_000_000, transcendentals=0, bytes_accessed=3 << 20),
        name="norm",
    )(hid, own, got, gain)


KC = 1024
DEPTH = 4
PDEPTH = 8


def mlp_kernel(*refs):
    xs, (wg, wu, wd), outs, (wbuf, dbuf, acc, sems, dsems) = refs[:4], refs[4:7], refs[7:10], refs[10:]
    nk = 4096 // KC
    ups = []
    for k in range(nk):
        rows = pl.ds(k * KC, KC)
        ups.append(
            (
                pltpu.make_async_copy(wg.at[rows], wbuf.at[k, :, pl.ds(0, 896)], sems.at[k, 0]),
                pltpu.make_async_copy(wu.at[rows], wbuf.at[k, :, pl.ds(896, 896)], sems.at[k, 1]),
            )
        )
    downs = [pltpu.make_async_copy(wd.at[:, pl.ds(n * 1024, 1024)], dbuf.at[n], dsems.at[n]) for n in range(4)]
    order = [d for pair in ups for d in pair] + downs
    for d in order[:DEPTH]:
        d.start()

    def settle(at, count):
        for i in range(at, at + count):
            order[i].wait()
        for i in range(at + DEPTH, min(at + DEPTH + count, len(order))):
            order[i].start()

    for k in range(nk):
        settle(2 * k, 2)
        a = jnp.concatenate([r[:, k * KC : (k + 1) * KC] for r in xs], axis=0)
        part = jnp.dot(a, wbuf[k], preferred_element_type=F32)
        if k == 0:
            acc[...] = part
        else:
            acc[...] += part
    gate = acc[:, :896]
    inner = (gate / (1.0 + jnp.exp(-gate)) * acc[:, 896:]).astype(BF)
    for n in range(4):
        settle(2 * nk + n, 1)
        res = jnp.dot(inner, dbuf[n], preferred_element_type=F32).astype(BF)
        lo = 0
        for o in outs:
            m = o.shape[0]
            o[:, n * 1024 : (n + 1) * 1024] = res[lo : lo + m]
            lo += m


def mlp(xs, wg, wu, wd):
    vm = pl.BlockSpec(memory_space=pltpu.VMEM)
    hb = pl.BlockSpec(memory_space=pltpu.HBM)
    return pl.pallas_call(
        mlp_kernel,
        in_specs=[vm] * 4 + [hb] * 3,
        out_specs=[vm] * 3,
        out_shape=[jax.ShapeDtypeStruct((n, 4096), BF) for n in (64, 128, 64)],
        scratch_shapes=[
            pltpu.VMEM((4096 // KC, KC, 1792), BF),
            pltpu.VMEM((4, 896, 1024), BF),
            pltpu.VMEM((256, 1792), F32),
            pltpu.SemaphoreType.DMA((4096 // KC, 2)),
            pltpu.SemaphoreType.DMA((4,)),
        ],
        compiler_params=pltpu.CompilerParams(vmem_limit_bytes=VLIM),
        cost_estimate=pl.CostEstimate(flops=5_640_000_000, transcendentals=0, bytes_accessed=26 << 20),
    )(*xs, wg, wu, wd)


def added(a, b):
    return (a.astype(F32) + b.astype(F32)).astype(BF)


def exchange_qkv(queries, key_states, value_states):
    both = jnp.concatenate(
        [queries.reshape(64, 8, 256), key_states.reshape(64, 8, 128), value_states.reshape(64, 8, 128)], axis=2
    )
    got = lax.all_to_all(both, "head", split_axis=1, concat_axis=0, tiled=True)
    got = got.reshape(512, 512)
    return got[:, :256], got[:, 256:]


def local(hidden_in, queries, key_states, value_states, out_weight, norm_gain, gate_weight, up_weight, down_weight):
    head = lax.axis_index("head")
    blk = lax.axis_index("blk")
    x, zl = head % 4, head // 4
    c, y, zh = blk % 2, (blk // 2) % 4, blk // 8

    q_own, kv = exchange_qkv(queries, key_states, value_states)

    steps = [(1, 0), (-1, 0), (0, 1), (2, 0), (1, 1), (-1, 1), (2, 1)]
    kvs, key_ids = [kv], [blk]
    for i, (dy, dz) in enumerate(steps):
        kvs.append(move(kv, blk_by(dy, dz)))
        key_ids.append((zh ^ dz) * 8 + ((y - dy) % 4) * 2 + c)
        if i == 2:
            q_oth = move(q_own, core_swap)
    key_ids = [jnp.asarray(v, jnp.int32) for v in key_ids]
    ids_a = jnp.stack(key_ids[:4] + [blk, blk ^ 1])
    ids_b = jnp.stack(key_ids[4:] + [blk, blk ^ 1])

    mine = lax.dynamic_slice_in_dim(out_weight, c * 128, 128, 0)
    rest = lax.dynamic_slice_in_dim(out_weight, (1 - c) * 128, 128, 0)
    g1a = move(mine, x_out)
    g1b = move(rest, x_out)
    g2 = move(g1a, x_out)
    s1a, s1b, s2 = (move(g1a, core_swap), move(g1b, core_swap), move(g2, core_swap))
    side = jnp.where(c == 0, -1, 1)
    w_ids = jnp.stack([jnp.asarray(v, jnp.int32) for v in (x, (x + side) % 4, (x - side) % 4, (x + 2) % 4, zl, c)])

    state = flash(ids_a, q_own, q_oth, kvs[:4], None, False)
    o_own, ml_own, o_oth, ml_oth = flash(ids_b, q_own, q_oth, kvs[4:], state, True)
    o_in, ml_in = move(o_oth, core_swap), move(ml_oth, core_swap)
    att = merge(o_own, ml_own, o_in, ml_in)
    att = lax.all_to_all(att, "head", split_axis=0, concat_axis=0, axis_index_groups=[[0, 1, 2, 3], [4, 5, 6, 7]], tiled=True)
    own_sum, oth_sum = project(w_ids, att, out_weight, [g1a, g1b, s1b, s1a, g2, s2])
    got_sum = move(oth_sum, z_low_pair)
    residual, normed = residual_norm(hidden_in, own_sum, got_sum, norm_gain.reshape(1, 4096))

    n_p = move(normed, x_by(-1))
    n_m = move(normed, x_by(1))
    n_2 = move(normed, x_by(2))
    z_0 = move(normed, z_pair)
    z_p = move(n_p, z_pair)
    z_m = move(n_m, z_pair)
    z_2 = move(n_2, z_pair)
    weights = (gate_weight, up_weight, down_weight)
    p_2, p_pm, p_0 = mlp([n_2, n_p, n_m, normed], *weights)
    f_2, f_pm, f_0 = mlp([z_2, z_p, z_m, z_0], *weights)
    h_2 = move(f_2, z_pair)
    h_pm = move(f_pm, z_pair)
    h_0 = move(f_0, z_pair)
    r_2 = move(added(p_2, h_2), x_by(2))
    r_p = move(added(p_pm[:64], h_pm[:64]), x_by(1))
    r_m = move(added(p_pm[64:], h_pm[64:]), x_by(-1))
    total = p_0.astype(F32) + h_0.astype(F32) + r_2.astype(F32) + r_p.astype(F32) + r_m.astype(F32)
    return (residual.astype(F32) + total).astype(BF)


def solution(mesh):
    tok = P(("blk", "head"), None)
    return jax.shard_map(
        local,
        mesh=mesh,
        in_specs=(tok, tok, tok, tok, P("head", None), P(), P(None, "head"), P(None, "head"), P("head", None)),
        out_specs=tok,
        check_vma=False,
    )
```

profile of v0, /device:TPU:120, one launch (start us, length us, event | category | flops | bytes accessed | tf_op | source)
XLA Modules:
  0.0 224.3 jit_solution(511318178242042107)
XLA Ops:
  0.0 3.2 %constant_dynamic-slice_fusion = (bf16[128,4096]{1,0:T(8,128)(2,1)}, bf16[128,4096]{1,0:T(8,128)(2,1)}) fusion(bf16[256,4096]{1,0:T(8,128)(2,1)} %own_w.1, s32[]{:T(128)S(6)} %select_n.84, s32[]{:T(128)S(6)} %select_n.83), kind=kLoop, calls=%fused_computation.8 | loop fusion | bytes 4194312 | tf_op jit(solution)/shard_map/dynamic_slice | solution.py:362
  7.4 5.5 %all-to-all-start = ((bf16[64,8,512]{2,0,1:T(8,128)(2,1)}), bf16[64,8,512]{2,0,1:T(8,128)(2,1)S(1)}, u32[]{:S(2)}, u32[]{:S(2)}) async-start(bf16[64,8,512]{2,0,1:T(8,128)(2,1)} %pad_maximum_fusion), calls=%async_computation | async-start | bytes 1048576 | tf_op jit(solution)/shard_map/all_to_all | solution.py:337
  14.4 7.8 %collective-permute-done.10.refs_0_ = bf16[128,4096]{1,0:T(8,128)(2,1)S(1)} collective-permute-done((bf16[128,4096]{1,0:T(8,128)(2,1)}, bf16[128,4096]{1,0:T(8,128)(2,1)S(1)}, u32[]{:S(2)}, u32[]{:S(2)}) %collective-permute-start.10) | collective-permute-done | bytes 1048608 | tf_op jit(solution)/shard_map/ppermute | solution.py:31
  22.5 2.4 %all-to-all-done = bf16[64,8,512]{2,0,1:T(8,128)(2,1)S(1)} async-done(((bf16[64,8,512]{2,0,1:T(8,128)(2,1)}), bf16[64,8,512]{2,0,1:T(8,128)(2,1)S(1)}, u32[]{:S(2)}, u32[]{:S(2)}) %all-to-all-start) | async-done | bytes 524320 | tf_op jit(solution)/shard_map/all_to_all | solution.py:337
  27.8 2.0 collective-permute-start.5
  29.8 6.3 %collective-permute-done.7.refs_3_ = bf16[512,256]{1,0:T(8,128)(2,1)} collective-permute-done((bf16[512,256]{1,0:T(8,128)(2,1)}, bf16[512,256]{1,0:T(8,128)(2,1)}, u32[]{:S(2)}, u32[]{:S(2)}) %collective-permute-start.7) | collective-permute-done | bytes 262176 | tf_op jit(solution)/shard_map/ppermute | solution.py:31
  37.1 2.5 %collective-permute-start.3 = (bf16[512,256]{1,0:T(8,128)(2,1)}, bf16[512,256]{1,0:T(8,128)(2,1)}, u32[]{:S(2)}, u32[]{:S(2)}) collective-permute-start(bf16[512,256]{1,0:T(8,128)(2,1)} %get-tuple-element.45.refs_0_), channel_id=1, source_target_pairs={{0,14},{1,15},{64,78},{65,79},{8,6},{9,7},{72,70},{73,71},{2,8},{3... | collective-permute-start | bytes 786440 | tf_op jit(solution)/shard_map/ppermute | solution.py:31
  40.9 3.1 %collective-permute-start.2 = (bf16[512,256]{1,0:T(8,128)(2,1)}, bf16[512,256]{1,0:T(8,128)(2,1)S(1)}, u32[]{:S(2)}, u32[]{:S(2)}) collective-permute-start(bf16[512,256]{1,0:T(8,128)(2,1)} %get-tuple-element.45.refs_0_), channel_id=1, source_target_pairs={{0,10},{1,11},{64,74},{65,75},{8,2},{9,3},{72,66},{73,67},{2,12},{... | collective-permute-start | bytes 786440 | tf_op jit(solution)/shard_map/ppermute | solution.py:31
  44.0 7.0 %collective-permute-done.4.refs_3_ = bf16[512,256]{1,0:T(8,128)(2,1)S(1)} collective-permute-done((bf16[512,256]{1,0:T(8,128)(2,1)}, bf16[512,256]{1,0:T(8,128)(2,1)S(1)}, u32[]{:S(2)}, u32[]{:S(2)}) %collective-permute-start.4) | collective-permute-done | bytes 262176 | tf_op jit(solution)/shard_map/ppermute | solution.py:31
  51.9 7.5 %collective-permute-done.3.refs_2_ = bf16[512,256]{1,0:T(8,128)(2,1)} collective-permute-done((bf16[512,256]{1,0:T(8,128)(2,1)}, bf16[512,256]{1,0:T(8,128)(2,1)}, u32[]{:S(2)}, u32[]{:S(2)}) %collective-permute-start.3) | collective-permute-done | bytes 262176 | tf_op jit(solution)/shard_map/ppermute | solution.py:31
  60.1 13.8 %shard_map.91 = (f32[512,256]{1,0:T(8,128)}, f32[512,128]{1,0:T(8,128)}, f32[512,256]{1,0:T(8,128)}, f32[512,128]{1,0:T(8,128)}) custom-call(s32[6]{0:T(128)} %stack.74.ids, bf16[512,256]{1,0:T(8,128)(2,1)} %copy-done.14, bf16[512,256]{1,0:T(8,128)(2,1)} %copy-done.17, bf16[512,256]{1,0:T(8,128)(2,1)} %get-tuple-element.45.refs_0_, ...), custom_call_target="tpu_custom_call" | custom-call | flops 4400000000 | bytes 4194304 | tf_op jit(solution)/shard_map/pallas_call | solution.py:135
  74.7 14.6 %shard_map.92 = (f32[512,256]{1,0:T(8,128)}, f32[512,128]{1,0:T(8,128)}, bf16[512,256]{1,0:T(8,128)(2,1)}, f32[512,128]{1,0:T(8,128)}) custom-call(s32[6]{0:T(128)} %stack.70.ids, bf16[512,256]{1,0:T(8,128)(2,1)} %copy-done.14, bf16[512,256]{1,0:T(8,128)(2,1)} %copy-done.17, bf16[512,256]{1,0:T(8,128)(2,1)} %copy-done.22, bf16[512,256]{1,0:T(8,128)(2,1)} %copy-done.21, ...), custom_call_target="tpu_custom_call" | custom-call | flops 4400000000 | bytes 4194304 | tf_op jit(solution)/shard_map/pallas_call | solution.py:135
  91.8 2.4 %merge.1 = bf16[4,2,64,256]{3,2,1,0:T(8,128)(2,1)} custom-call(f32[512,256]{1,0:T(8,128)} %get-tuple-element.27.o_own, f32[512,128]{1,0:T(8,128)} %get-tuple-element.28.ml_own, bf16[512,256]{1,0:T(8,128)(2,1)} %copy-done.15, f32[512,128]{1,0:T(8,128)} %collective-permute-done.9.ml_in), custom_call_target="tpu_custom_call" | custom-call | flops 1000000 | bytes 1048576 | tf_op jit(solution)/shard_map/merge/pallas_call | solution.py:176
  94.1 3.6 %all-to-all-start.1 = ((bf16[4,2,64,256]{3,2,1,0:T(8,128)(2,1)}), bf16[4,2,64,256]{3,2,1,0:T(8,128)(2,1)S(1)}, u32[]{:S(2)}, u32[]{:S(2)}) async-start(bf16[4,2,64,256]{3,2,1,0:T(8,128)(2,1)} %merge.1), calls=%async_computation.1 | async-start | bytes 524288 | tf_op jit(solution)/shard_map/all_to_all | solution.py:374
  98.4 6.4 %all-to-all-done.1.att = bf16[4,2,64,256]{3,2,1,0:T(8,128)(2,1)S(1)} async-done(((bf16[4,2,64,256]{3,2,1,0:T(8,128)(2,1)}), bf16[4,2,64,256]{3,2,1,0:T(8,128)(2,1)S(1)}, u32[]{:S(2)}, u32[]{:S(2)}) %all-to-all-start.1) | async-done | bytes 262176 | tf_op jit(solution)/shard_map/all_to_all | solution.py:374
  105.9 6.0 %project.1 = (f32[64,4096]{1,0:T(8,128)}, bf16[64,4096]{1,0:T(8,128)(2,1)}) custom-call(s32[6]{0:T(128)} %stack.63.ids, bf16[4,2,64,256]{3,2,1,0:T(8,128)(2,1)} %copy-done.4, bf16[256,4096]{1,0:T(8,128)(2,1)} %own_w.1, bf16[128,4096]{1,0:T(8,128)(2,1)} %copy-done.1, bf16[128,4096]{1,0:T(8,128)(2,1)} %copy-done.2, ...), custom_call_target="tpu_custom_call" | custom-call | flops 1100000000 | bytes 9437184 | tf_op jit(solution)/shard_map/project/pallas_call | solution.py:225
  111.9 1.7 collective-permute-start.16
  113.6 11.4 %collective-permute-done.16.got = bf16[64,4096]{1,0:T(8,128)(2,1)S(1)} collective-permute-done((bf16[64,4096]{1,0:T(8,128)(2,1)}, bf16[64,4096]{1,0:T(8,128)(2,1)S(1)}, u32[]{:S(2)}, u32[]{:S(2)}) %collective-permute-start.16) | collective-permute-done | bytes 524320 | tf_op jit(solution)/shard_map/ppermute | solution.py:31
  125.8 2.8 %norm.1 = (bf16[64,4096]{1,0:T(8,128)(2,1)}, bf16[64,4096]{1,0:T(8,128)(2,1)}) custom-call(bf16[64,4096]{1,0:T(8,128)(2,1)} %hid.1, f32[64,4096]{1,0:T(8,128)} %get-tuple-element.31.own, bf16[64,4096]{1,0:T(8,128)(2,1)} %copy-done.13, f32[1,4096]{1,0:T(1,128)} %bitcast.38), custom_call_target="tpu_custom_call" | custom-call | flops 2000000 | bytes 3145728 | tf_op jit(solution)/shard_map/norm/pallas_call | solution.py:251
  129.2 2.7 %collective-permute-start.18 = (bf16[64,4096]{1,0:T(8,128)(2,1)}, bf16[64,4096]{1,0:T(8,128)(2,1)S(1)}, u32[]{:S(2)}, u32[]{:S(2)}) collective-permute-start(bf16[64,4096]{1,0:T(8,128)(2,1)} %get-tuple-element.34.refs_3_), channel_id=1, source_target_pairs={{0,48},{1,49},{64,112},{65,113},{8,56},{9,57},{72,120},{73,121},{2... | collective-permute-start | bytes 1572872 | tf_op jit(solution)/shard_map/ppermute | solution.py:31
  133.5 19.7 %collective-permute-done.19.refs_2_ = bf16[64,4096]{1,0:T(8,128)(2,1)S(1)} collective-permute-done((bf16[64,4096]{1,0:T(8,128)(2,1)}, bf16[64,4096]{1,0:T(8,128)(2,1)S(1)}, u32[]{:S(2)}, u32[]{:S(2)}) %collective-permute-start.19) | collective-permute-done | bytes 524320 | tf_op jit(solution)/shard_map/ppermute | solution.py:31
  156.9 5.5 %collective-permute-done.22.refs_2_ = bf16[64,4096]{1,0:T(8,128)(2,1)S(1)} collective-permute-done((bf16[64,4096]{1,0:T(8,128)(2,1)S(1)}, bf16[64,4096]{1,0:T(8,128)(2,1)S(1)}, u32[]{:S(2)}, u32[]{:S(2)}) %collective-permute-start.22) | collective-permute-done | bytes 524320 | tf_op jit(solution)/shard_map/ppermute | solution.py:31
  162.4 5.6 %collective-permute-done.21.refs_1_ = bf16[64,4096]{1,0:T(8,128)(2,1)S(1)} collective-permute-done((bf16[64,4096]{1,0:T(8,128)(2,1)S(1)}, bf16[64,4096]{1,0:T(8,128)(2,1)S(1)}, u32[]{:S(2)}, u32[]{:S(2)}) %collective-permute-start.21) | collective-permute-done | bytes 524320 | tf_op jit(solution)/shard_map/ppermute | solution.py:31
  168.0 5.6 %collective-permute-done.20.refs_0_ = bf16[64,4096]{1,0:T(8,128)(2,1)S(1)} collective-permute-done((bf16[64,4096]{1,0:T(8,128)(2,1)S(1)}, bf16[64,4096]{1,0:T(8,128)(2,1)S(1)}, u32[]{:S(2)}, u32[]{:S(2)}) %collective-permute-start.20) | collective-permute-done | bytes 524320 | tf_op jit(solution)/shard_map/ppermute | solution.py:31
  174.4 13.1 %shard_map.94 = (bf16[64,4096]{1,0:T(8,128)(2,1)}, bf16[128,4096]{1,0:T(8,128)(2,1)}, bf16[64,4096]{1,0:T(8,128)(2,1)}) custom-call(bf16[64,4096]{1,0:T(8,128)(2,1)} %copy-done.12, bf16[64,4096]{1,0:T(8,128)(2,1)} %copy-done.11, bf16[64,4096]{1,0:T(8,128)(2,1)} %copy-done.10, bf16[64,4096]{1,0:T(8,128)(2,1)} %copy-done.9, bf16[4096,896]{1,0:T(8,128)(2,1)} %refs_4_.3, ...), custom_call_target="tpu_custom_call" | custom-call | flops 5640000000 | bytes 27262976 | tf_op jit(solution)/shard_map/pallas_call | solution.py:312
  187.6 1.7 collective-permute-start.25
  189.7 13.1 %shard_map.93 = (bf16[64,4096]{1,0:T(8,128)(2,1)}, bf16[128,4096]{1,0:T(8,128)(2,1)}, bf16[64,4096]{1,0:T(8,128)(2,1)}) custom-call(bf16[64,4096]{1,0:T(8,128)(2,1)} %copy-done.8, bf16[64,4096]{1,0:T(8,128)(2,1)} %copy-done.7, bf16[64,4096]{1,0:T(8,128)(2,1)} %copy-done.6, bf16[64,4096]{1,0:T(8,128)(2,1)} %get-tuple-element.34.refs_3_, ...), custom_call_target="tpu_custom_call" | custom-call | flops 5640000000 | bytes 27262976 | tf_op jit(solution)/shard_map/pallas_call | solution.py:312
  205.7 2.5 %collective-permute-done.27 = bf16[128,4096]{1,0:T(8,128)(2,1)S(1)} collective-permute-done((bf16[128,4096]{1,0:T(8,128)(2,1)}, bf16[128,4096]{1,0:T(8,128)(2,1)S(1)}, u32[]{:S(2)}, u32[]{:S(2)}) %collective-permute-start.27) | collective-permute-done | bytes 1048608 | tf_op jit(solution)/shard_map/ppermute | solution.py:31
  209.8 3.2 %collective-permute-start.29 = (bf16[64,4096]{1,0:T(8,128)(2,1)S(1)}, bf16[64,4096]{1,0:T(8,128)(2,1)S(1)}, u32[]{:S(2)}, u32[]{:S(2)}) collective-permute-start(bf16[64,4096]{1,0:T(8,128)(2,1)S(1)} %get-tuple-element.42), channel_id=1, source_target_pairs={{0,48},{1,49},{64,112},{65,113},{8,56},{9,57},{72,120},{73,121},{2... | collective-permute-start | bytes 1572872 | tf_op jit(solution)/shard_map/ppermute | solution.py:31
  213.9 2.6 %collective-permute-done.26 = bf16[64,4096]{1,0:T(8,128)(2,1)S(1)} collective-permute-done((bf16[64,4096]{1,0:T(8,128)(2,1)S(1)}, bf16[64,4096]{1,0:T(8,128)(2,1)S(1)}, u32[]{:S(2)}, u32[]{:S(2)}) %collective-permute-start.26) | collective-permute-done | bytes 524320 | tf_op jit(solution)/shard_map/ppermute | solution.py:31
  216.5 5.5 %collective-permute-done.28 = bf16[64,4096]{1,0:T(8,128)(2,1)S(1)} collective-permute-done((bf16[64,4096]{1,0:T(8,128)(2,1)S(1)}, bf16[64,4096]{1,0:T(8,128)(2,1)S(1)}, u32[]{:S(2)}, u32[]{:S(2)}) %collective-permute-start.28) | collective-permute-done | bytes 524320 | tf_op jit(solution)/shard_map/ppermute | solution.py:31
  222.0 2.2 %add_convert_fusion = bf16[64,4096]{1,0:T(8,128)(2,1)} fusion(bf16[64,4096]{1,0:T(8,128)(2,1)S(1)} %collective-permute-done.29, bf16[64,4096]{1,0:T(8,128)(2,1)S(1)} %collective-permute-done.28, bf16[64,4096]{1,0:T(8,128)(2,1)S(1)} %collective-permute-done.26, bf16[64,4096]{1,0:T(8,128)(2,1)S(1)} %collective-permute-done.24, ...), kind=kLoop, calls=%fused_computation | loop fusion | flops 3145728 | bytes 3670016 | tf_op jit(solution)/shard_map/convert_element_type | solution.py:396
  (96 shorter events, 30.9 us)
Async XLA Ops:
  3.2 19.0 %collective-permute-start.10 = (bf16[128,4096]{1,0:T(8,128)(2,1)}, bf16[128,4096]{1,0:T(8,128)(2,1)S(1)}, u32[]{:S(2)}, u32[]{:S(2)}) collective-permute-start(bf16[128,4096]{1,0:T(8,128)(2,1)} %get-tuple-element.44), channel_id=1, source_target_pairs={{0,16},{1,49},{64,80},{65,113},{8,24},{9,57},{72,88},{73,121},{2,1... | collective-permute-start | bytes 3145736 | tf_op jit(solution)/shard_map/ppermute | solution.py:31
  7.4 17.4 %all-to-all-start = ((bf16[64,8,512]{2,0,1:T(8,128)(2,1)}), bf16[64,8,512]{2,0,1:T(8,128)(2,1)S(1)}, u32[]{:S(2)}, u32[]{:S(2)}) async-start(bf16[64,8,512]{2,0,1:T(8,128)(2,1)} %pad_maximum_fusion), calls=%async_computation | async-start | bytes 1048576 | tf_op jit(solution)/shard_map/all_to_all | solution.py:337
  12.9 46.5 %collective-permute-start.11 = (bf16[128,4096]{1,0:T(8,128)(2,1)}, bf16[128,4096]{1,0:T(8,128)(2,1)S(1)}, u32[]{:S(2)}, u32[]{:S(2)}) collective-permute-start(bf16[128,4096]{1,0:T(8,128)(2,1)} %get-tuple-element.43), channel_id=1, source_target_pairs={{0,16},{1,49},{64,80},{65,113},{8,24},{9,57},{72,88},{73,121},{2,1... | collective-permute-start | bytes 3145736 | tf_op jit(solution)/shard_map/ppermute | solution.py:31
  22.2 37.8 %collective-permute-start.14 = (bf16[128,4096]{1,0:T(8,128)(2,1)S(1)}, bf16[128,4096]{1,0:T(8,128)(2,1)}, u32[]{:S(2)}, u32[]{:S(2)}) collective-permute-start(bf16[128,4096]{1,0:T(8,128)(2,1)S(1)} %collective-permute-done.10.refs_0_), channel_id=1, source_target_pairs={{0,16},{1,49},{64,80},{65,113},{8,24},{9,57},{72,88},{73,121},{2,1... | collective-permute-start | bytes 3145736 | tf_op jit(solution)/shard_map/ppermute | solution.py:31
  25.6 1.5 collective-permute-start
  25.6 10.5 %collective-permute-start.7 = (bf16[512,256]{1,0:T(8,128)(2,1)}, bf16[512,256]{1,0:T(8,128)(2,1)}, u32[]{:S(2)}, u32[]{:S(2)}) collective-permute-start(bf16[512,256]{1,0:T(8,128)(2,1)} %get-tuple-element.45.refs_0_), channel_id=1, source_target_pairs={{0,8},{1,9},{64,72},{65,73},{8,0},{9,1},{72,64},{73,65},{2,10},{3,... | collective-permute-start | bytes 786440 | tf_op jit(solution)/shard_map/ppermute | solution.py:31
  25.8 11.2 %collective-permute-start.6 = (bf16[512,256]{1,0:T(8,128)(2,1)}, bf16[512,256]{1,0:T(8,128)(2,1)S(1)}, u32[]{:S(2)}, u32[]{:S(2)}) collective-permute-start(bf16[512,256]{1,0:T(8,128)(2,1)} %get-tuple-element.45.refs_0_), channel_id=1, source_target_pairs={{0,6},{1,7},{64,70},{65,71},{8,14},{9,15},{72,78},{73,79},{2,0},{3... | collective-permute-start | bytes 786440 | tf_op jit(solution)/shard_map/ppermute | solution.py:31
  27.8 13.1 %collective-permute-start.5 = (bf16[512,256]{1,0:T(8,128)(2,1)}, bf16[512,256]{1,0:T(8,128)(2,1)S(1)}, u32[]{:S(2)}, u32[]{:S(2)}) collective-permute-start(bf16[512,256]{1,0:T(8,128)(2,1)} %get-tuple-element.45.refs_0_), channel_id=1, source_target_pairs={{0,2},{1,3},{64,66},{65,67},{8,10},{9,11},{72,74},{73,75},{2,4},{3... | collective-permute-start | bytes 786440 | tf_op jit(solution)/shard_map/ppermute | solution.py:31
  36.1 14.8 %collective-permute-start.4 = (bf16[512,256]{1,0:T(8,128)(2,1)}, bf16[512,256]{1,0:T(8,128)(2,1)S(1)}, u32[]{:S(2)}, u32[]{:S(2)}) collective-permute-start(bf16[512,256]{1,0:T(8,128)(2,1)} %get-tuple-element.45.refs_0_), channel_id=1, source_target_pairs={{0,12},{1,13},{64,76},{65,77},{8,4},{9,5},{72,68},{73,69},{2,14},{... | collective-permute-start | bytes 786440 | tf_op jit(solution)/shard_map/ppermute | solution.py:31
  37.1 22.4 %collective-permute-start.3 = (bf16[512,256]{1,0:T(8,128)(2,1)}, bf16[512,256]{1,0:T(8,128)(2,1)}, u32[]{:S(2)}, u32[]{:S(2)}) collective-permute-start(bf16[512,256]{1,0:T(8,128)(2,1)} %get-tuple-element.45.refs_0_), channel_id=1, source_target_pairs={{0,14},{1,15},{64,78},{65,79},{8,6},{9,7},{72,70},{73,71},{2,8},{3... | collective-permute-start | bytes 786440 | tf_op jit(solution)/shard_map/ppermute | solution.py:31
  40.9 33.0 %collective-permute-start.2 = (bf16[512,256]{1,0:T(8,128)(2,1)}, bf16[512,256]{1,0:T(8,128)(2,1)S(1)}, u32[]{:S(2)}, u32[]{:S(2)}) collective-permute-start(bf16[512,256]{1,0:T(8,128)(2,1)} %get-tuple-element.45.refs_0_), channel_id=1, source_target_pairs={{0,10},{1,11},{64,74},{65,75},{8,2},{9,3},{72,66},{73,67},{2,12},{... | collective-permute-start | bytes 786440 | tf_op jit(solution)/shard_map/ppermute | solution.py:31
  51.0 22.9 %collective-permute-start.1 = (bf16[512,256]{1,0:T(8,128)(2,1)}, bf16[512,256]{1,0:T(8,128)(2,1)S(1)}, u32[]{:S(2)}, u32[]{:S(2)}) collective-permute-start(bf16[512,256]{1,0:T(8,128)(2,1)} %get-tuple-element.45.refs_0_), channel_id=1, source_target_pairs={{0,4},{1,5},{64,68},{65,69},{8,12},{9,13},{72,76},{73,77},{2,6},{3... | collective-permute-start | bytes 786440 | tf_op jit(solution)/shard_map/ppermute | solution.py:31
  59.4 45.3 %collective-permute-start.13 = (bf16[128,4096]{1,0:T(8,128)(2,1)S(1)}, bf16[128,4096]{1,0:T(8,128)(2,1)S(1)}, u32[]{:S(2)}, u32[]{:S(2)}) collective-permute-start(bf16[128,4096]{1,0:T(8,128)(2,1)S(1)} %collective-permute-done.10.refs_0_), channel_id=1, source_target_pairs={{0,1},{1,0},{64,65},{65,64},{8,9},{9,8},{72,73},{73,72},{2,3},{3,2... | collective-permute-start | bytes 3145736 | tf_op jit(solution)/shard_map/ppermute | solution.py:31
  59.5 45.3 %collective-permute-start.12 = (bf16[128,4096]{1,0:T(8,128)(2,1)S(1)}, bf16[128,4096]{1,0:T(8,128)(2,1)}, u32[]{:S(2)}, u32[]{:S(2)}) collective-permute-start(bf16[128,4096]{1,0:T(8,128)(2,1)S(1)} %collective-permute-done.11.refs_1_), channel_id=1, source_target_pairs={{0,1},{1,0},{64,65},{65,64},{8,9},{9,8},{72,73},{73,72},{2,3},{3,2... | collective-permute-start | bytes 3145736 | tf_op jit(solution)/shard_map/ppermute | solution.py:31
  60.0 44.8 %collective-permute-start.15 = (bf16[128,4096]{1,0:T(8,128)(2,1)}, bf16[128,4096]{1,0:T(8,128)(2,1)}, u32[]{:S(2)}, u32[]{:S(2)}) collective-permute-start(bf16[128,4096]{1,0:T(8,128)(2,1)} %collective-permute-done.14.refs_4_), channel_id=1, source_target_pairs={{0,1},{1,0},{64,65},{65,64},{8,9},{9,8},{72,73},{73,72},{2,3},{3,2... | collective-permute-start | bytes 3145736 | tf_op jit(solution)/shard_map/ppermute | solution.py:31
  89.3 1.7 collective-permute-start.8
  89.3 2.2 %collective-permute-start.9 = (f32[512,128]{1,0:T(8,128)}, f32[512,128]{1,0:T(8,128)}, u32[]{:S(2)}, u32[]{:S(2)}) collective-permute-start(f32[512,128]{1,0:T(8,128)} %get-tuple-element.30), channel_id=1, source_target_pairs={{0,1},{1,0},{64,65},{65,64},{8,9},{9,8},{72,73},{73,72},{2,3},{3,2... | collective-permute-start | bytes 786440 | tf_op jit(solution)/shard_map/ppermute | solution.py:31
  94.1 10.6 %all-to-all-start.1 = ((bf16[4,2,64,256]{3,2,1,0:T(8,128)(2,1)}), bf16[4,2,64,256]{3,2,1,0:T(8,128)(2,1)S(1)}, u32[]{:S(2)}, u32[]{:S(2)}) async-start(bf16[4,2,64,256]{3,2,1,0:T(8,128)(2,1)} %merge.1), calls=%async_computation.1 | async-start | bytes 524288 | tf_op jit(solution)/shard_map/all_to_all | solution.py:374
  111.9 13.1 %collective-permute-start.16 = (bf16[64,4096]{1,0:T(8,128)(2,1)}, bf16[64,4096]{1,0:T(8,128)(2,1)S(1)}, u32[]{:S(2)}, u32[]{:S(2)}) collective-permute-start(bf16[64,4096]{1,0:T(8,128)(2,1)} %get-tuple-element.32), channel_id=1, source_target_pairs={{0,64},{1,65},{64,0},{65,1},{8,72},{9,73},{72,8},{73,9},{2,66},{3,... | collective-permute-start | bytes 1572872 | tf_op jit(solution)/shard_map/ppermute | solution.py:31
  128.6 24.6 %collective-permute-start.19 = (bf16[64,4096]{1,0:T(8,128)(2,1)}, bf16[64,4096]{1,0:T(8,128)(2,1)S(1)}, u32[]{:S(2)}, u32[]{:S(2)}) collective-permute-start(bf16[64,4096]{1,0:T(8,128)(2,1)} %get-tuple-element.34.refs_3_), channel_id=1, source_target_pairs={{0,16},{1,17},{64,80},{65,81},{8,24},{9,25},{72,88},{73,89},{2,18}... | collective-permute-start | bytes 1572872 | tf_op jit(solution)/shard_map/ppermute | solution.py:31
  129.2 25.7 %collective-permute-start.18 = (bf16[64,4096]{1,0:T(8,128)(2,1)}, bf16[64,4096]{1,0:T(8,128)(2,1)S(1)}, u32[]{:S(2)}, u32[]{:S(2)}) collective-permute-start(bf16[64,4096]{1,0:T(8,128)(2,1)} %get-tuple-element.34.refs_3_), channel_id=1, source_target_pairs={{0,48},{1,49},{64,112},{65,113},{8,56},{9,57},{72,120},{73,121},{2... | collective-permute-start | bytes 1572872 | tf_op jit(solution)/shard_map/ppermute | solution.py:31
  131.8 23.4 %collective-permute-start.17 = (bf16[64,4096]{1,0:T(8,128)(2,1)}, bf16[64,4096]{1,0:T(8,128)(2,1)S(1)}, u32[]{:S(2)}, u32[]{:S(2)}) collective-permute-start(bf16[64,4096]{1,0:T(8,128)(2,1)} %get-tuple-element.34.refs_3_), channel_id=1, source_target_pairs={{0,32},{1,33},{64,96},{65,97},{8,40},{9,41},{72,104},{73,105},{2,3... | collective-permute-start | bytes 1572872 | tf_op jit(solution)/shard_map/ppermute | solution.py:31
  131.8 25.0 %collective-permute-start.23 = (bf16[64,4096]{1,0:T(8,128)(2,1)}, bf16[64,4096]{1,0:T(8,128)(2,1)S(1)}, u32[]{:S(2)}, u32[]{:S(2)}) collective-permute-start(bf16[64,4096]{1,0:T(8,128)(2,1)} %get-tuple-element.34.refs_3_), channel_id=1, source_target_pairs={{0,64},{1,73},{64,0},{65,9},{8,72},{9,65},{72,8},{73,1},{2,66},{3,... | collective-permute-start | bytes 1572872 | tf_op jit(solution)/shard_map/ppermute | solution.py:31
  153.2 9.2 %collective-permute-start.22 = (bf16[64,4096]{1,0:T(8,128)(2,1)S(1)}, bf16[64,4096]{1,0:T(8,128)(2,1)S(1)}, u32[]{:S(2)}, u32[]{:S(2)}) collective-permute-start(bf16[64,4096]{1,0:T(8,128)(2,1)S(1)} %collective-permute-done.19.refs_2_), channel_id=1, source_target_pairs={{0,64},{1,73},{64,0},{65,9},{8,72},{9,65},{72,8},{73,1},{2,66},{3,... | collective-permute-start | bytes 1572872 | tf_op jit(solution)/shard_map/ppermute | solution.py:31
  154.8 13.2 %collective-permute-start.21 = (bf16[64,4096]{1,0:T(8,128)(2,1)S(1)}, bf16[64,4096]{1,0:T(8,128)(2,1)S(1)}, u32[]{:S(2)}, u32[]{:S(2)}) collective-permute-start(bf16[64,4096]{1,0:T(8,128)(2,1)S(1)} %collective-permute-done.18.refs_1_), channel_id=1, source_target_pairs={{0,64},{1,73},{64,0},{65,9},{8,72},{9,65},{72,8},{73,1},{2,66},{3,... | collective-permute-start | bytes 1572872 | tf_op jit(solution)/shard_map/ppermute | solution.py:31
  155.2 18.4 %collective-permute-start.20 = (bf16[64,4096]{1,0:T(8,128)(2,1)S(1)}, bf16[64,4096]{1,0:T(8,128)(2,1)S(1)}, u32[]{:S(2)}, u32[]{:S(2)}) collective-permute-start(bf16[64,4096]{1,0:T(8,128)(2,1)S(1)} %collective-permute-done.17.refs_0_), channel_id=1, source_target_pairs={{0,64},{1,73},{64,0},{65,9},{8,72},{9,65},{72,8},{73,1},{2,66},{3,... | collective-permute-start | bytes 1572872 | tf_op jit(solution)/shard_map/ppermute | solution.py:31
  187.6 16.9 %collective-permute-start.25 = (bf16[64,4096]{1,0:T(8,128)(2,1)}, bf16[64,4096]{1,0:T(8,128)(2,1)S(1)}, u32[]{:S(2)}, u32[]{:S(2)}) collective-permute-start(bf16[64,4096]{1,0:T(8,128)(2,1)} %get-tuple-element.38), channel_id=1, source_target_pairs={{0,64},{1,73},{64,0},{65,9},{8,72},{9,65},{72,8},{73,1},{2,66},{3,... | collective-permute-start | bytes 1572872 | tf_op jit(solution)/shard_map/ppermute | solution.py:31
  189.3 19.0 %collective-permute-start.27 = (bf16[128,4096]{1,0:T(8,128)(2,1)}, bf16[128,4096]{1,0:T(8,128)(2,1)S(1)}, u32[]{:S(2)}, u32[]{:S(2)}) collective-permute-start(bf16[128,4096]{1,0:T(8,128)(2,1)} %get-tuple-element.40), channel_id=1, source_target_pairs={{0,64},{1,73},{64,0},{65,9},{8,72},{9,65},{72,8},{73,1},{2,66},{3,... | collective-permute-start | bytes 3145736 | tf_op jit(solution)/shard_map/ppermute | solution.py:31
  202.8 11.1 %collective-permute-start.24 = (bf16[64,4096]{1,0:T(8,128)(2,1)S(1)}, bf16[64,4096]{1,0:T(8,128)(2,1)S(1)}, u32[]{:S(2)}, u32[]{:S(2)}) collective-permute-start(bf16[64,4096]{1,0:T(8,128)(2,1)S(1)} %copy-done.16), channel_id=1, source_target_pairs={{0,64},{1,73},{64,0},{65,9},{8,72},{9,65},{72,8},{73,1},{2,66},{3,... | collective-permute-start | bytes 1572872 | tf_op jit(solution)/shard_map/ppermute | solution.py:31
  205.6 10.9 %collective-permute-start.26 = (bf16[64,4096]{1,0:T(8,128)(2,1)S(1)}, bf16[64,4096]{1,0:T(8,128)(2,1)S(1)}, u32[]{:S(2)}, u32[]{:S(2)}) collective-permute-start(bf16[64,4096]{1,0:T(8,128)(2,1)S(1)} %add_convert_fusion.3), channel_id=1, source_target_pairs={{0,32},{1,33},{64,96},{65,97},{8,40},{9,41},{72,104},{73,105},{2,3... | collective-permute-start | bytes 1572872 | tf_op jit(solution)/shard_map/ppermute | solution.py:31
  209.7 12.3 %collective-permute-start.28 = (bf16[64,4096]{1,0:T(8,128)(2,1)S(1)}, bf16[64,4096]{1,0:T(8,128)(2,1)S(1)}, u32[]{:S(2)}, u32[]{:S(2)}) collective-permute-start(bf16[64,4096]{1,0:T(8,128)(2,1)S(1)} %get-tuple-element.41), channel_id=1, source_target_pairs={{0,16},{1,17},{64,80},{65,81},{8,24},{9,25},{72,88},{73,89},{2,18}... | collective-permute-start | bytes 1572872 | tf_op jit(solution)/shard_map/ppermute | solution.py:31
  209.8 12.2 %collective-permute-start.29 = (bf16[64,4096]{1,0:T(8,128)(2,1)S(1)}, bf16[64,4096]{1,0:T(8,128)(2,1)S(1)}, u32[]{:S(2)}, u32[]{:S(2)}) collective-permute-start(bf16[64,4096]{1,0:T(8,128)(2,1)S(1)} %get-tuple-element.42), channel_id=1, source_target_pairs={{0,48},{1,49},{64,112},{65,113},{8,56},{9,57},{72,120},{73,121},{2... | collective-permute-start | bytes 1572872 | tf_op jit(solution)/shard_map/ppermute | solution.py:31
  (23 other events, 318.6 us)
where the time goes:
time: 225 us; the launch traced here: 224 us
  waiting for transfers between devices  99.1 us (44%)
  Pallas kernels  65.8 us (29%)
  starting transfers between devices  41.3 us (18%)
  local copies, waits for them, and re-layouts  12 us (5%)
  other arithmetic  5.7 us (3%)
    ppermute x30, waiting for transfers between devices, move(): return lax.ppermute(a, ('head', 'blk'), pairs)  90.3 us
    ppermute x30, starting transfers between devices, move(): return lax.ppermute(a, ('head', 'blk'), pairs)  32.3 us
    pallas_call x2, Pallas kernels, flash(): pl.pallas_call(functools.partial(flash_kernel, n, init is None), in_specs...  28.4 us
    pallas_call x2, Pallas kernels, mlp(): pl.pallas_call(mlp_kernel, in_specs=[vm] * 4 + [hb] * 3, out_specs=[vm] *...  26.2 us
    all_to_all x1, waiting for transfers between devices, local(): lax.all_to_all(att, 'head', split_axis=0, concat_axis=0, axis_index_group...  6.39 us
    pallas_call x1, Pallas kernels, project(): pl.pallas_call(proj_outer, in_specs=[pl.BlockSpec(memory_space=pltpu.SMEM...  6.01 us
    all_to_all x1, starting transfers between devices, exchange_qkv(): got = lax.all_to_all(both, 'head', split_axis=1, concat_axis=0, tiled=True)  5.47 us
  transfers between devices with their start and end apart: 32, of which 18 were waited for; matrix products, arithmetic and copies ran while one was open for 4% of the time, Pallas kernels for 20%

commit v1 on v0

--- a/solution.py
+++ b/solution.py
@@ -39,6 +39,10 @@
     return (x + 1 if c == 0 else x - 1, y, z, c)
 
 
+def x_in(x, y, z, c):
+    return (x - 1 if c == 0 else x + 1, y, z, c)
+
+
 def core_swap(x, y, z, c):
     return (x, y, z, 1 - c)
 
@@ -55,24 +59,36 @@
     return lambda x, y, z, c: (x, y + dy, z + 2 * dz, c)
 
 
-ROWS = 256
-
-
-def flash_body(q2, k, va, m_ref, acc_ref, qi, mask):
+ROWS = 128
+
+
+GROUP = 2
+
+
+def flash_body(q2, kk, va, m_ref, acc_ref, qi, slots, mask):
     for h in range(2):
         for r in range(512 // ROWS):
             rows = pl.ds(r * ROWS, ROWS)
             q = q2[qi, rows, h * 128 : (h + 1) * 128]
-            s = lax.dot_general(q, k, (((1,), (1,)), ((), ())), preferred_element_type=F32)
-            if mask:
-                ri = lax.broadcasted_iota(jnp.int32, s.shape, 0) + r * ROWS
-                ci = lax.broadcasted_iota(jnp.int32, s.shape, 1)
-                s = jnp.where(ci <= ri, s, NEG)
+            ss = []
+            for j in slots:
+                s = lax.dot_general(q, kk[j], (((1,), (1,)), ((), ())), preferred_element_type=F32)
+                if mask:
+                    ri = lax.broadcasted_iota(jnp.int32, s.shape, 0) + r * ROWS
+                    ci = lax.broadcasted_iota(jnp.int32, s.shape, 1)
+                    s = jnp.where(ci <= ri, s, NEG)
+                ss.append(s)
+            top = ss[0]
+            for s in ss[1:]:
+                top = jnp.maximum(top, s)
             m_old = m_ref[qi, h, rows, :]
-            m_new = jnp.maximum(m_old, jnp.max(s, axis=-1, keepdims=True) * SCALE2)
-            p = jnp.exp2(s * SCALE2 - m_new[:, :1]).astype(BF)
+            m_new = jnp.maximum(m_old, jnp.max(top, axis=-1, keepdims=True) * SCALE2)
+            pv = None
+            for j, s in zip(slots, ss):
+                p = jnp.exp2(s * SCALE2 - m_new[:, :1]).astype(BF)
+                part = jnp.dot(p, va[j], preferred_element_type=F32)
+                pv = part if pv is None else pv + part
             alpha = jnp.exp2(m_old - m_new)
-            pv = jnp.dot(p, va, preferred_element_type=F32)
             acc = acc_ref[qi, h, rows, :]
             acc_ref[qi, h, rows, :] = acc * jnp.concatenate([alpha, alpha], axis=1) + pv
             m_ref[qi, h, rows, :] = m_new
@@ -82,7 +98,7 @@
     kvs, refs = refs[:n], refs[n:]
     if not first:
         init, refs = refs[:4], refs[4:]
-    outs, (q2, kk, va, m_ref, acc_ref) = refs[:4], refs[4:]
+    outs, (q2, kk, va, m_ref, acc_ref, vis) = refs[:4], refs[4:]
     q2[0] = q_own[...]
     q2[1] = q_oth[...]
     for j in range(n):
@@ -92,7 +108,7 @@
     if first:
         m_ref[...] = jnp.full(m_ref.shape, NEG, F32)
         acc_ref[...] = jnp.zeros(acc_ref.shape, F32)
-        flash_body(q2, kk[0], va[0], m_ref, acc_ref, 0, True)
+        flash_body(q2, kk, va, m_ref, acc_ref, 0, [0], True)
     else:
         for qi in range(2):
             for h in range(2):
@@ -101,19 +117,31 @@
                 acc_ref[qi, h, :, :128] = init[2 * qi][:, h * 128 : (h + 1) * 128]
                 acc_ref[qi, h, :, 128:] = jnp.where(lse > NEG, 1.0, 0.0)
 
-    lead = 1 if first else 0
-
-    def step(t, carry):
-        qi = (t >= n - lead).astype(jnp.int32)
-        j = t - qi * (n - lead) + lead * (1 - qi)
-
-        @pl.when(ids[j] < ids[n + qi])
-        def _():
-            flash_body(q2, kk[j], va[j], m_ref, acc_ref, qi, False)
-
+    counts = []
+    for qi in range(2):
+        seen = jnp.int32(0)
+        for j in range(n):
+            vis[qi, seen] = j
+            seen = seen + (ids[j] < ids[n + qi]).astype(jnp.int32)
+        counts.append(seen)
+    groups = [cnt // GROUP for cnt in counts]
+
+    def grouped(t, carry):
+        qi = (t >= groups[0]).astype(jnp.int32)
+        at = (t - qi * groups[0]) * GROUP
+        flash_body(q2, kk, va, m_ref, acc_ref, qi, [vis[qi, at + g] for g in range(GROUP)], False)
         return carry
 
-    lax.fori_loop(0, 2 * n - lead, step, 0)
+    lax.fori_loop(0, groups[0] + groups[1], grouped, 0)
+    rest = [cnt - g * GROUP for cnt, g in zip(counts, groups)]
+
+    def single(t, carry):
+        qi = (t >= rest[0]).astype(jnp.int32)
+        at = jnp.where(qi == 1, groups[1], groups[0]) * GROUP + t - qi * rest[0]
+        flash_body(q2, kk, va, m_ref, acc_ref, qi, [vis[qi, at]], False)
+        return carry
+
+    lax.fori_loop(0, rest[0] + rest[1], single, 0)
     lane = lax.broadcasted_iota(jnp.int32, (512, 128), 1)
     for qi in range(2):
         o_ref, ml = outs[2 * qi], outs[2 * qi + 1]
@@ -148,6 +176,7 @@
             pltpu.VMEM((n, 512, 256), BF),
             pltpu.VMEM((2, 2, 512, 128), F32),
             pltpu.VMEM((2, 2, 512, 256), F32),
+            pltpu.SMEM((2, n + 1), jnp.int32),
         ],
         compiler_params=pltpu.CompilerParams(vmem_limit_bytes=VLIM),
         cost_estimate=pl.CostEstimate(flops=1_100_000_000 * n, transcendentals=0, bytes_accessed=4 << 20),
@@ -264,7 +293,7 @@
 
 
 def mlp_kernel(*refs):
-    xs, (wg, wu, wd), outs, (wbuf, dbuf, acc, sems, dsems) = refs[:4], refs[4:7], refs[7:10], refs[10:]
+    xs, (wg, wu, wd), outs, (wbuf, dbuf, acc, sems, dsems) = refs[:4], refs[4:7], refs[7:11], refs[11:]
     nk = 4096 // KC
     ups = []
     for k in range(nk):
@@ -312,8 +341,8 @@
     return pl.pallas_call(
         mlp_kernel,
         in_specs=[vm] * 4 + [hb] * 3,
-        out_specs=[vm] * 3,
-        out_shape=[jax.ShapeDtypeStruct((n, 4096), BF) for n in (64, 128, 64)],
+        out_specs=[vm] * 4,
+        out_shape=[jax.ShapeDtypeStruct((64, 4096), BF)] * 4,
         scratch_shapes=[
             pltpu.VMEM((4096 // KC, KC, 1792), BF),
             pltpu.VMEM((4, 896, 1024), BF),
@@ -330,11 +359,24 @@
     return (a.astype(F32) + b.astype(F32)).astype(BF)
 
 
+def pack_kernel(q, k, v, out):
+    for h in range(8):
+        out[h, :, :256] = q[:, h * 256 : (h + 1) * 256]
+        out[h, :, 256:384] = k[:, h * 128 : (h + 1) * 128]
+        out[h, :, 384:] = v[:, h * 128 : (h + 1) * 128]
+
+
 def exchange_qkv(queries, key_states, value_states):
-    both = jnp.concatenate(
-        [queries.reshape(64, 8, 256), key_states.reshape(64, 8, 128), value_states.reshape(64, 8, 128)], axis=2
-    )
-    got = lax.all_to_all(both, "head", split_axis=1, concat_axis=0, tiled=True)
+    vm = pl.BlockSpec(memory_space=pltpu.VMEM)
+    both = pl.pallas_call(
+        pack_kernel,
+        in_specs=[vm] * 3,
+        out_specs=vm,
+        out_shape=jax.ShapeDtypeStruct((8, 64, 512), BF),
+        cost_estimate=pl.CostEstimate(flops=1_000_000, transcendentals=0, bytes_accessed=1 << 20),
+        name="pack",
+    )(queries, key_states, value_states)
+    got = lax.all_to_all(both, "head", split_axis=0, concat_axis=0, tiled=True)
     got = got.reshape(512, 512)
     return got[:, :256], got[:, 256:]
 
@@ -371,28 +413,31 @@
     o_own, ml_own, o_oth, ml_oth = flash(ids_b, q_own, q_oth, kvs[4:], state, True)
     o_in, ml_in = move(o_oth, core_swap), move(ml_oth, core_swap)
     att = merge(o_own, ml_own, o_in, ml_in)
-    att = lax.all_to_all(att, "head", split_axis=0, concat_axis=0, axis_index_groups=[[0, 1, 2, 3], [4, 5, 6, 7]], tiled=True)
+    att = lax.all_to_all(
+        att, "head", split_axis=0, concat_axis=0, axis_index_groups=[[0, 1, 2, 3], [4, 5, 6, 7]], tiled=True
+    )
     own_sum, oth_sum = project(w_ids, att, out_weight, [g1a, g1b, s1b, s1a, g2, s2])
     got_sum = move(oth_sum, z_low_pair)
     residual, normed = residual_norm(hidden_in, own_sum, got_sum, norm_gain.reshape(1, 4096))
 
-    n_p = move(normed, x_by(-1))
-    n_m = move(normed, x_by(1))
-    n_2 = move(normed, x_by(2))
+    n_a = move(normed, x_out)
+    n_b = move(normed, x_in)
     z_0 = move(normed, z_pair)
-    z_p = move(n_p, z_pair)
-    z_m = move(n_m, z_pair)
+    n_2 = move(n_a, x_out)
+    z_a = move(n_a, z_pair)
+    z_b = move(n_b, z_pair)
     z_2 = move(n_2, z_pair)
     weights = (gate_weight, up_weight, down_weight)
-    p_2, p_pm, p_0 = mlp([n_2, n_p, n_m, normed], *weights)
-    f_2, f_pm, f_0 = mlp([z_2, z_p, z_m, z_0], *weights)
+    p_0, p_a, p_b, f_0 = mlp([normed, n_a, n_b, z_0], *weights)
+    h_0 = move(f_0, z_pair)
+    f_2, f_a, f_b, p_2 = mlp([z_2, z_a, z_b, n_2], *weights)
     h_2 = move(f_2, z_pair)
-    h_pm = move(f_pm, z_pair)
-    h_0 = move(f_0, z_pair)
+    h_a = move(f_a, z_pair)
+    h_b = move(f_b, z_pair)
     r_2 = move(added(p_2, h_2), x_by(2))
-    r_p = move(added(p_pm[:64], h_pm[:64]), x_by(1))
-    r_m = move(added(p_pm[64:], h_pm[64:]), x_by(-1))
-    total = p_0.astype(F32) + h_0.astype(F32) + r_2.astype(F32) + r_p.astype(F32) + r_m.astype(F32)
+    r_a = move(added(p_a, h_a), x_in)
+    r_b = move(added(p_b, h_b), x_out)
+    total = p_0.astype(F32) + h_0.astype(F32) + r_2.astype(F32) + r_a.astype(F32) + r_b.astype(F32)
     return (residual.astype(F32) + total).astype(BF)
 
 

time: 225 us -> 223 us (level)
  the two profiles are of different devices: /device:TPU:120 before, /device:TPU:88 now
where the time goes in v1:
time: 223 us
  waiting for transfers between devices  105 us (47%)
  Pallas kernels  61.6 us (28%)
  starting transfers between devices  40.4 us (18%)
  local copies, waits for them, and re-layouts  10.9 us (5%)
  other arithmetic  4.69 us (2%)
    ppermute x31, waiting for transfers between devices, move(): return lax.ppermute(a, ('head', 'blk'), pairs)  94.5 us
    ppermute x31, starting transfers between devices, move(): return lax.ppermute(a, ('head', 'blk'), pairs)  31.9 us
    pallas_call x2, Pallas kernels, mlp(): pl.pallas_call(mlp_kernel, in_specs=[vm] * 4 + [hb] * 3, out_specs=[vm] *...  26.2 us
    pallas_call x2, Pallas kernels, flash(): pl.pallas_call(functools.partial(flash_kernel, n, init is None), in_specs...  22.3 us
    all_to_all x1, waiting for transfers between devices, local(): lax.all_to_all(att, 'head', split_axis=0, concat_axis=0, axis_index_group...  6.8 us
    pallas_call x1, Pallas kernels, project(): pl.pallas_call(proj_outer, in_specs=[pl.BlockSpec(memory_space=pltpu.SMEM...  6 us
    unnamed x48, local copies, waits for them, and re-layouts  5.17 us
    all_to_all x1, starting transfers between devices, exchange_qkv(): got = lax.all_to_all(both, 'head', split_axis=0, concat_axis=0, tiled=True)  5.07 us
  transfers between devices with their start and end apart: 33, of which 18 were waited for; matrix products, arithmetic and copies ran while one was open for 2% of the time, Pallas kernels for 24%

profile of v1, /device:TPU:88, one launch (start us, length us, event | category | flops | bytes accessed | tf_op | source)
XLA Modules:
  0.0 222.8 jit_solution(2183480663051610328)
XLA Ops:
  0.0 3.1 %constant_dynamic-slice_fusion = (bf16[128,4096]{1,0:T(8,128)(2,1)}, bf16[128,4096]{1,0:T(8,128)(2,1)}) fusion(bf16[256,4096]{1,0:T(8,128)(2,1)} %own_w.1, s32[]{:T(128)S(6)} %select_n.84, s32[]{:T(128)S(6)} %select_n.83), kind=kLoop, calls=%fused_computation.4 | loop fusion | bytes 4194312 | tf_op jit(solution)/shard_map/dynamic_slice | solution.py:404
  4.6 1.9 pack.1
  6.5 5.1 %all-to-all-start = ((bf16[8,64,512]{2,1,0:T(8,128)(2,1)}), bf16[8,64,512]{2,1,0:T(8,128)(2,1)S(1)}, u32[]{:S(2)}, u32[]{:S(2)}) async-start(bf16[8,64,512]{2,1,0:T(8,128)(2,1)} %pack.1), calls=%async_computation | async-start | bytes 1048576 | tf_op jit(solution)/shard_map/all_to_all | solution.py:379
  11.6 2.0 collective-permute-start.11
  13.6 8.5 %collective-permute-done.10.refs_0_ = bf16[128,4096]{1,0:T(8,128)(2,1)S(1)} collective-permute-done((bf16[128,4096]{1,0:T(8,128)(2,1)}, bf16[128,4096]{1,0:T(8,128)(2,1)S(1)}, u32[]{:S(2)}, u32[]{:S(2)}) %collective-permute-start.10) | collective-permute-done | bytes 1048608 | tf_op jit(solution)/shard_map/ppermute | solution.py:31
  22.4 3.6 %all-to-all-done = bf16[8,64,512]{2,1,0:T(8,128)(2,1)S(1)} async-done(((bf16[8,64,512]{2,1,0:T(8,128)(2,1)}), bf16[8,64,512]{2,1,0:T(8,128)(2,1)S(1)}, u32[]{:S(2)}, u32[]{:S(2)}) %all-to-all-start) | async-done | bytes 524320 | tf_op jit(solution)/shard_map/all_to_all | solution.py:379
  29.0 1.8 collective-permute-start.5
  30.8 6.5 %collective-permute-done.7.refs_3_ = bf16[512,256]{1,0:T(8,128)(2,1)} collective-permute-done((bf16[512,256]{1,0:T(8,128)(2,1)}, bf16[512,256]{1,0:T(8,128)(2,1)}, u32[]{:S(2)}, u32[]{:S(2)}) %collective-permute-start.7) | collective-permute-done | bytes 262176 | tf_op jit(solution)/shard_map/ppermute | solution.py:31
  38.3 2.5 %collective-permute-start.3 = (bf16[512,256]{1,0:T(8,128)(2,1)}, bf16[512,256]{1,0:T(8,128)(2,1)}, u32[]{:S(2)}, u32[]{:S(2)}) collective-permute-start(bf16[512,256]{1,0:T(8,128)(2,1)} %get-tuple-element.47.refs_0_), channel_id=1, source_target_pairs={{0,14},{1,15},{64,78},{65,79},{8,6},{9,7},{72,70},{73,71},{2,8},{3... | collective-permute-start | bytes 786440 | tf_op jit(solution)/shard_map/ppermute | solution.py:31
  42.1 3.1 %collective-permute-start.2 = (bf16[512,256]{1,0:T(8,128)(2,1)}, bf16[512,256]{1,0:T(8,128)(2,1)S(1)}, u32[]{:S(2)}, u32[]{:S(2)}) collective-permute-start(bf16[512,256]{1,0:T(8,128)(2,1)} %get-tuple-element.47.refs_0_), channel_id=1, source_target_pairs={{0,10},{1,11},{64,74},{65,75},{8,2},{9,3},{72,66},{73,67},{2,12},{... | collective-permute-start | bytes 786440 | tf_op jit(solution)/shard_map/ppermute | solution.py:31
  45.2 7.0 %collective-permute-done.4.refs_3_ = bf16[512,256]{1,0:T(8,128)(2,1)S(1)} collective-permute-done((bf16[512,256]{1,0:T(8,128)(2,1)}, bf16[512,256]{1,0:T(8,128)(2,1)S(1)}, u32[]{:S(2)}, u32[]{:S(2)}) %collective-permute-start.4) | collective-permute-done | bytes 262176 | tf_op jit(solution)/shard_map/ppermute | solution.py:31
  53.1 7.5 %collective-permute-done.3.refs_2_ = bf16[512,256]{1,0:T(8,128)(2,1)} collective-permute-done((bf16[512,256]{1,0:T(8,128)(2,1)}, bf16[512,256]{1,0:T(8,128)(2,1)}, u32[]{:S(2)}, u32[]{:S(2)}) %collective-permute-start.3) | collective-permute-done | bytes 262176 | tf_op jit(solution)/shard_map/ppermute | solution.py:31
  61.2 11.6 %shard_map.91 = (f32[512,256]{1,0:T(8,128)}, f32[512,128]{1,0:T(8,128)}, f32[512,256]{1,0:T(8,128)}, f32[512,128]{1,0:T(8,128)}) custom-call(s32[6]{0:T(128)} %stack.74.ids, bf16[512,256]{1,0:T(8,128)(2,1)} %copy-done.14, bf16[512,256]{1,0:T(8,128)(2,1)} %copy-done.18, bf16[512,256]{1,0:T(8,128)(2,1)} %get-tuple-element.47.refs_0_, ...), custom_call_target="tpu_custom_call" | custom-call | flops 4400000000 | bytes 4194304 | tf_op jit(solution)/shard_map/pallas_call | solution.py:163
  73.6 10.7 %shard_map.92 = (f32[512,256]{1,0:T(8,128)}, f32[512,128]{1,0:T(8,128)}, bf16[512,256]{1,0:T(8,128)(2,1)}, f32[512,128]{1,0:T(8,128)}) custom-call(s32[6]{0:T(128)} %stack.70.ids, bf16[512,256]{1,0:T(8,128)(2,1)} %copy-done.14, bf16[512,256]{1,0:T(8,128)(2,1)} %copy-done.18, bf16[512,256]{1,0:T(8,128)(2,1)} %copy-done.23, bf16[512,256]{1,0:T(8,128)(2,1)} %copy-done.22, ...), custom_call_target="tpu_custom_call" | custom-call | flops 4400000000 | bytes 4194304 | tf_op jit(solution)/shard_map/pallas_call | solution.py:163
  87.0 2.4 %merge.1 = bf16[4,2,64,256]{3,2,1,0:T(8,128)(2,1)} custom-call(f32[512,256]{1,0:T(8,128)} %get-tuple-element.29.o_own, f32[512,128]{1,0:T(8,128)} %get-tuple-element.30.ml_own, bf16[512,256]{1,0:T(8,128)(2,1)} %copy-done.15, f32[512,128]{1,0:T(8,128)} %collective-permute-done.9.ml_in), custom_call_target="tpu_custom_call" | custom-call | flops 1000000 | bytes 1048576 | tf_op jit(solution)/shard_map/merge/pallas_call | solution.py:205
  89.3 3.4 %all-to-all-start.1 = ((bf16[4,2,64,256]{3,2,1,0:T(8,128)(2,1)}), bf16[4,2,64,256]{3,2,1,0:T(8,128)(2,1)S(1)}, u32[]{:S(2)}, u32[]{:S(2)}) async-start(bf16[4,2,64,256]{3,2,1,0:T(8,128)(2,1)} %merge.1), calls=%async_computation.1 | async-start | bytes 524288 | tf_op jit(solution)/shard_map/all_to_all | solution.py:416
  93.4 6.8 %all-to-all-done.1.att = bf16[4,2,64,256]{3,2,1,0:T(8,128)(2,1)S(1)} async-done(((bf16[4,2,64,256]{3,2,1,0:T(8,128)(2,1)}), bf16[4,2,64,256]{3,2,1,0:T(8,128)(2,1)S(1)}, u32[]{:S(2)}, u32[]{:S(2)}) %all-to-all-start.1) | async-done | bytes 262176 | tf_op jit(solution)/shard_map/all_to_all | solution.py:416
  101.3 6.0 %project.1 = (f32[64,4096]{1,0:T(8,128)}, bf16[64,4096]{1,0:T(8,128)(2,1)}) custom-call(s32[6]{0:T(128)} %stack.63.ids, bf16[4,2,64,256]{3,2,1,0:T(8,128)(2,1)} %copy-done.3, bf16[256,4096]{1,0:T(8,128)(2,1)} %own_w.1, bf16[128,4096]{1,0:T(8,128)(2,1)} %copy-done, bf16[128,4096]{1,0:T(8,128)(2,1)} %copy-done.1, ...), custom_call_target="tpu_custom_call" | custom-call | flops 1100000000 | bytes 9437184 | tf_op jit(solution)/shard_map/project/pallas_call | solution.py:254
  107.8 13.2 %collective-permute-done.16.got = bf16[64,4096]{1,0:T(8,128)(2,1)S(1)} collective-permute-done((bf16[64,4096]{1,0:T(8,128)(2,1)}, bf16[64,4096]{1,0:T(8,128)(2,1)S(1)}, u32[]{:S(2)}, u32[]{:S(2)}) %collective-permute-start.16) | collective-permute-done | bytes 524320 | tf_op jit(solution)/shard_map/ppermute | solution.py:31
  121.8 2.8 %norm.1 = (bf16[64,4096]{1,0:T(8,128)(2,1)}, bf16[64,4096]{1,0:T(8,128)(2,1)}) custom-call(bf16[64,4096]{1,0:T(8,128)(2,1)} %hid.1, f32[64,4096]{1,0:T(8,128)} %get-tuple-element.33.own, bf16[64,4096]{1,0:T(8,128)(2,1)} %copy-done.13, f32[1,4096]{1,0:T(1,128)} %bitcast.18), custom_call_target="tpu_custom_call" | custom-call | flops 2000000 | bytes 3145728 | tf_op jit(solution)/shard_map/norm/pallas_call | solution.py:280
  125.1 2.7 %collective-permute-start.18 = (bf16[64,4096]{1,0:T(8,128)(2,1)}, bf16[64,4096]{1,0:T(8,128)(2,1)S(1)}, u32[]{:S(2)}, u32[]{:S(2)}) collective-permute-start(bf16[64,4096]{1,0:T(8,128)(2,1)} %get-tuple-element.36.refs_0_), channel_id=1, source_target_pairs={{0,48},{1,17},{64,112},{65,81},{8,56},{9,25},{72,120},{73,89},{2,5... | collective-permute-start | bytes 1572872 | tf_op jit(solution)/shard_map/ppermute | solution.py:31
  127.8 11.5 %collective-permute-done.17.refs_1_ = bf16[64,4096]{1,0:T(8,128)(2,1)S(1)} collective-permute-done((bf16[64,4096]{1,0:T(8,128)(2,1)}, bf16[64,4096]{1,0:T(8,128)(2,1)S(1)}, u32[]{:S(2)}, u32[]{:S(2)}) %collective-permute-start.17) | collective-permute-done | bytes 524320 | tf_op jit(solution)/shard_map/ppermute | solution.py:31
  141.4 8.4 %collective-permute-done.21.refs_3_ = bf16[64,4096]{1,0:T(8,128)(2,1)S(1)} collective-permute-done((bf16[64,4096]{1,0:T(8,128)(2,1)S(1)}, bf16[64,4096]{1,0:T(8,128)(2,1)S(1)}, u32[]{:S(2)}, u32[]{:S(2)}) %collective-permute-start.21) | collective-permute-done | bytes 524320 | tf_op jit(solution)/shard_map/ppermute | solution.py:31
  151.8 2.4 %collective-permute-done.24.refs_2_ = bf16[64,4096]{1,0:T(8,128)(2,1)S(1)} collective-permute-done((bf16[64,4096]{1,0:T(8,128)(2,1)S(1)}, bf16[64,4096]{1,0:T(8,128)(2,1)S(1)}, u32[]{:S(2)}, u32[]{:S(2)}) %collective-permute-start.24) | collective-permute-done | bytes 524320 | tf_op jit(solution)/shard_map/ppermute | solution.py:31
  154.2 5.6 %collective-permute-done.22.refs_0_ = bf16[64,4096]{1,0:T(8,128)(2,1)S(1)} collective-permute-done((bf16[64,4096]{1,0:T(8,128)(2,1)S(1)}, bf16[64,4096]{1,0:T(8,128)(2,1)S(1)}, u32[]{:S(2)}, u32[]{:S(2)}) %collective-permute-start.22) | collective-permute-done | bytes 524320 | tf_op jit(solution)/shard_map/ppermute | solution.py:31
  160.6 13.1 %shard_map.94 = (bf16[64,4096]{1,0:T(8,128)(2,1)}, bf16[64,4096]{1,0:T(8,128)(2,1)}, bf16[64,4096]{1,0:T(8,128)(2,1)}, bf16[64,4096]{1,0:T(8,128)(2,1)}) custom-call(bf16[64,4096]{1,0:T(8,128)(2,1)} %copy-done.12, bf16[64,4096]{1,0:T(8,128)(2,1)} %copy-done.9, bf16[64,4096]{1,0:T(8,128)(2,1)} %copy-done.11, bf16[64,4096]{1,0:T(8,128)(2,1)} %copy-done.8, ...), custom_call_target="tpu_custom_call" | custom-call | flops 5640000000 | bytes 27262976 | tf_op jit(solution)/shard_map/pallas_call | solution.py:341
  175.0 13.1 %shard_map.93 = (bf16[64,4096]{1,0:T(8,128)(2,1)}, bf16[64,4096]{1,0:T(8,128)(2,1)}, bf16[64,4096]{1,0:T(8,128)(2,1)}, bf16[64,4096]{1,0:T(8,128)(2,1)}) custom-call(bf16[64,4096]{1,0:T(8,128)(2,1)} %get-tuple-element.36.refs_0_, bf16[64,4096]{1,0:T(8,128)(2,1)} %copy-done.5, bf16[64,4096]{1,0:T(8,128)(2,1)} %copy-done.6, bf16[64,4096]{1,0:T(8,128)(2,1)} %copy-done.10, ...), custom_call_target="tpu_custom_call" | custom-call | flops 5640000000 | bytes 27262976 | tf_op jit(solution)/shard_map/pallas_call | solution.py:341
  193.2 10.0 %collective-permute-done.27 = bf16[64,4096]{1,0:T(8,128)(2,1)S(1)} collective-permute-done((bf16[64,4096]{1,0:T(8,128)(2,1)S(1)}, bf16[64,4096]{1,0:T(8,128)(2,1)S(1)}, u32[]{:S(2)}, u32[]{:S(2)}) %collective-permute-start.27) | collective-permute-done | bytes 524320 | tf_op jit(solution)/shard_map/ppermute | solution.py:31
  204.4 3.3 %collective-permute-start.28 = (bf16[64,4096]{1,0:T(8,128)(2,1)S(1)}, bf16[64,4096]{1,0:T(8,128)(2,1)S(1)}, u32[]{:S(2)}, u32[]{:S(2)}) collective-permute-start(bf16[64,4096]{1,0:T(8,128)(2,1)S(1)} %add_convert_fusion.2), channel_id=1, source_target_pairs={{0,48},{1,17},{64,112},{65,81},{8,56},{9,25},{72,120},{73,89},{2,5... | collective-permute-start | bytes 1572872 | tf_op jit(solution)/shard_map/ppermute | solution.py:31
  210.3 7.2 %collective-permute-done.28 = bf16[64,4096]{1,0:T(8,128)(2,1)S(1)} collective-permute-done((bf16[64,4096]{1,0:T(8,128)(2,1)S(1)}, bf16[64,4096]{1,0:T(8,128)(2,1)S(1)}, u32[]{:S(2)}, u32[]{:S(2)}) %collective-permute-start.28) | collective-permute-done | bytes 524320 | tf_op jit(solution)/shard_map/ppermute | solution.py:31
  217.6 3.0 %collective-permute-done.30 = bf16[64,4096]{1,0:T(8,128)(2,1)S(1)} collective-permute-done((bf16[64,4096]{1,0:T(8,128)(2,1)S(1)}, bf16[64,4096]{1,0:T(8,128)(2,1)S(1)}, u32[]{:S(2)}, u32[]{:S(2)}) %collective-permute-start.30) | collective-permute-done | bytes 524320 | tf_op jit(solution)/shard_map/ppermute | solution.py:31
  220.5 2.2 %add_convert_fusion = bf16[64,4096]{1,0:T(8,128)(2,1)} fusion(bf16[64,4096]{1,0:T(8,128)(2,1)S(1)} %collective-permute-done.30, bf16[64,4096]{1,0:T(8,128)(2,1)S(1)} %collective-permute-done.28, bf16[64,4096]{1,0:T(8,128)(2,1)S(1)} %collective-permute-done.26, bf16[64,4096]{1,0:T(8,128)(2,1)S(1)} %collective-permute-done.20, ...), kind=kLoop, calls=%fused_computation | loop fusion | flops 3145728 | bytes 3670016 | tf_op jit(solution)/shard_map/convert_element_type | solution.py:441
  (99 shorter events, 30.4 us)
Async XLA Ops:
  3.1 19.0 %collective-permute-start.10 = (bf16[128,4096]{1,0:T(8,128)(2,1)}, bf16[128,4096]{1,0:T(8,128)(2,1)S(1)}, u32[]{:S(2)}, u32[]{:S(2)}) collective-permute-start(bf16[128,4096]{1,0:T(8,128)(2,1)} %get-tuple-element.46), channel_id=1, source_target_pairs={{0,16},{1,49},{64,80},{65,113},{8,24},{9,57},{72,88},{73,121},{2,1... | collective-permute-start | bytes 3145736 | tf_op jit(solution)/shard_map/ppermute | solution.py:31
  6.5 19.5 %all-to-all-start = ((bf16[8,64,512]{2,1,0:T(8,128)(2,1)}), bf16[8,64,512]{2,1,0:T(8,128)(2,1)S(1)}, u32[]{:S(2)}, u32[]{:S(2)}) async-start(bf16[8,64,512]{2,1,0:T(8,128)(2,1)} %pack.1), calls=%async_computation | async-start | bytes 1048576 | tf_op jit(solution)/shard_map/all_to_all | solution.py:379
  11.6 49.1 %collective-permute-start.11 = (bf16[128,4096]{1,0:T(8,128)(2,1)}, bf16[128,4096]{1,0:T(8,128)(2,1)S(1)}, u32[]{:S(2)}, u32[]{:S(2)}) collective-permute-start(bf16[128,4096]{1,0:T(8,128)(2,1)} %get-tuple-element.45), channel_id=1, source_target_pairs={{0,16},{1,49},{64,80},{65,113},{8,24},{9,57},{72,88},{73,121},{2,1... | collective-permute-start | bytes 3145736 | tf_op jit(solution)/shard_map/ppermute | solution.py:31
  22.1 39.0 %collective-permute-start.14 = (bf16[128,4096]{1,0:T(8,128)(2,1)S(1)}, bf16[128,4096]{1,0:T(8,128)(2,1)}, u32[]{:S(2)}, u32[]{:S(2)}) collective-permute-start(bf16[128,4096]{1,0:T(8,128)(2,1)S(1)} %collective-permute-done.10.refs_0_), channel_id=1, source_target_pairs={{0,16},{1,49},{64,80},{65,113},{8,24},{9,57},{72,88},{73,121},{2,1... | collective-permute-start | bytes 3145736 | tf_op jit(solution)/shard_map/ppermute | solution.py:31
  26.8 10.5 %collective-permute-start.7 = (bf16[512,256]{1,0:T(8,128)(2,1)}, bf16[512,256]{1,0:T(8,128)(2,1)}, u32[]{:S(2)}, u32[]{:S(2)}) collective-permute-start(bf16[512,256]{1,0:T(8,128)(2,1)} %get-tuple-element.47.refs_0_), channel_id=1, source_target_pairs={{0,8},{1,9},{64,72},{65,73},{8,0},{9,1},{72,64},{73,65},{2,10},{3,... | collective-permute-start | bytes 786440 | tf_op jit(solution)/shard_map/ppermute | solution.py:31
  26.8 11.5 %collective-permute-start.6 = (bf16[512,256]{1,0:T(8,128)(2,1)}, bf16[512,256]{1,0:T(8,128)(2,1)S(1)}, u32[]{:S(2)}, u32[]{:S(2)}) collective-permute-start(bf16[512,256]{1,0:T(8,128)(2,1)} %get-tuple-element.47.refs_0_), channel_id=1, source_target_pairs={{0,6},{1,7},{64,70},{65,71},{8,14},{9,15},{72,78},{73,79},{2,0},{3... | collective-permute-start | bytes 786440 | tf_op jit(solution)/shard_map/ppermute | solution.py:31
  29.0 13.1 %collective-permute-start.5 = (bf16[512,256]{1,0:T(8,128)(2,1)}, bf16[512,256]{1,0:T(8,128)(2,1)S(1)}, u32[]{:S(2)}, u32[]{:S(2)}) collective-permute-start(bf16[512,256]{1,0:T(8,128)(2,1)} %get-tuple-element.47.refs_0_), channel_id=1, source_target_pairs={{0,2},{1,3},{64,66},{65,67},{8,10},{9,11},{72,74},{73,75},{2,4},{3... | collective-permute-start | bytes 786440 | tf_op jit(solution)/shard_map/ppermute | solution.py:31
  37.3 14.8 %collective-permute-start.4 = (bf16[512,256]{1,0:T(8,128)(2,1)}, bf16[512,256]{1,0:T(8,128)(2,1)S(1)}, u32[]{:S(2)}, u32[]{:S(2)}) collective-permute-start(bf16[512,256]{1,0:T(8,128)(2,1)} %get-tuple-element.47.refs_0_), channel_id=1, source_target_pairs={{0,12},{1,13},{64,76},{65,77},{8,4},{9,5},{72,68},{73,69},{2,14},{... | collective-permute-start | bytes 786440 | tf_op jit(solution)/shard_map/ppermute | solution.py:31
  38.3 22.4 %collective-permute-start.3 = (bf16[512,256]{1,0:T(8,128)(2,1)}, bf16[512,256]{1,0:T(8,128)(2,1)}, u32[]{:S(2)}, u32[]{:S(2)}) collective-permute-start(bf16[512,256]{1,0:T(8,128)(2,1)} %get-tuple-element.47.refs_0_), channel_id=1, source_target_pairs={{0,14},{1,15},{64,78},{65,79},{8,6},{9,7},{72,70},{73,71},{2,8},{3... | collective-permute-start | bytes 786440 | tf_op jit(solution)/shard_map/ppermute | solution.py:31
  42.1 30.7 %collective-permute-start.2 = (bf16[512,256]{1,0:T(8,128)(2,1)}, bf16[512,256]{1,0:T(8,128)(2,1)S(1)}, u32[]{:S(2)}, u32[]{:S(2)}) collective-permute-start(bf16[512,256]{1,0:T(8,128)(2,1)} %get-tuple-element.47.refs_0_), channel_id=1, source_target_pairs={{0,10},{1,11},{64,74},{65,75},{8,2},{9,3},{72,66},{73,67},{2,12},{... | collective-permute-start | bytes 786440 | tf_op jit(solution)/shard_map/ppermute | solution.py:31
  52.2 20.7 %collective-permute-start.1 = (bf16[512,256]{1,0:T(8,128)(2,1)}, bf16[512,256]{1,0:T(8,128)(2,1)S(1)}, u32[]{:S(2)}, u32[]{:S(2)}) collective-permute-start(bf16[512,256]{1,0:T(8,128)(2,1)} %get-tuple-element.47.refs_0_), channel_id=1, source_target_pairs={{0,4},{1,5},{64,68},{65,69},{8,12},{9,13},{72,76},{73,77},{2,6},{3... | collective-permute-start | bytes 786440 | tf_op jit(solution)/shard_map/ppermute | solution.py:31
  60.6 39.6 %collective-permute-start.13 = (bf16[128,4096]{1,0:T(8,128)(2,1)S(1)}, bf16[128,4096]{1,0:T(8,128)(2,1)S(1)}, u32[]{:S(2)}, u32[]{:S(2)}) collective-permute-start(bf16[128,4096]{1,0:T(8,128)(2,1)S(1)} %collective-permute-done.10.refs_0_), channel_id=1, source_target_pairs={{0,1},{1,0},{64,65},{65,64},{8,9},{9,8},{72,73},{73,72},{2,3},{3,2... | collective-permute-start | bytes 3145736 | tf_op jit(solution)/shard_map/ppermute | solution.py:31
  60.6 39.6 %collective-permute-start.12 = (bf16[128,4096]{1,0:T(8,128)(2,1)S(1)}, bf16[128,4096]{1,0:T(8,128)(2,1)}, u32[]{:S(2)}, u32[]{:S(2)}) collective-permute-start(bf16[128,4096]{1,0:T(8,128)(2,1)S(1)} %collective-permute-done.11.refs_1_), channel_id=1, source_target_pairs={{0,1},{1,0},{64,65},{65,64},{8,9},{9,8},{72,73},{73,72},{2,3},{3,2... | collective-permute-start | bytes 3145736 | tf_op jit(solution)/shard_map/ppermute | solution.py:31
  61.1 39.1 %collective-permute-start.15 = (bf16[128,4096]{1,0:T(8,128)(2,1)}, bf16[128,4096]{1,0:T(8,128)(2,1)}, u32[]{:S(2)}, u32[]{:S(2)}) collective-permute-start(bf16[128,4096]{1,0:T(8,128)(2,1)} %collective-permute-done.14.refs_4_), channel_id=1, source_target_pairs={{0,1},{1,0},{64,65},{65,64},{8,9},{9,8},{72,73},{73,72},{2,3},{3,2... | collective-permute-start | bytes 3145736 | tf_op jit(solution)/shard_map/ppermute | solution.py:31
  84.3 1.9 collective-permute-start.8
  84.9 1.9 collective-permute-start.9
  89.3 10.9 %all-to-all-start.1 = ((bf16[4,2,64,256]{3,2,1,0:T(8,128)(2,1)}), bf16[4,2,64,256]{3,2,1,0:T(8,128)(2,1)S(1)}, u32[]{:S(2)}, u32[]{:S(2)}) async-start(bf16[4,2,64,256]{3,2,1,0:T(8,128)(2,1)} %merge.1), calls=%async_computation.1 | async-start | bytes 524288 | tf_op jit(solution)/shard_map/all_to_all | solution.py:416
  107.3 13.7 %collective-permute-start.16 = (bf16[64,4096]{1,0:T(8,128)(2,1)}, bf16[64,4096]{1,0:T(8,128)(2,1)S(1)}, u32[]{:S(2)}, u32[]{:S(2)}) collective-permute-start(bf16[64,4096]{1,0:T(8,128)(2,1)} %get-tuple-element.34), channel_id=1, source_target_pairs={{0,64},{1,65},{64,0},{65,1},{8,72},{9,73},{72,8},{73,9},{2,66},{3,... | collective-permute-start | bytes 1572872 | tf_op jit(solution)/shard_map/ppermute | solution.py:31
  124.6 14.8 %collective-permute-start.17 = (bf16[64,4096]{1,0:T(8,128)(2,1)}, bf16[64,4096]{1,0:T(8,128)(2,1)S(1)}, u32[]{:S(2)}, u32[]{:S(2)}) collective-permute-start(bf16[64,4096]{1,0:T(8,128)(2,1)} %get-tuple-element.36.refs_0_), channel_id=1, source_target_pairs={{0,16},{1,49},{64,80},{65,113},{8,24},{9,57},{72,88},{73,121},{2,1... | collective-permute-start | bytes 1572872 | tf_op jit(solution)/shard_map/ppermute | solution.py:31
  125.1 14.6 %collective-permute-start.18 = (bf16[64,4096]{1,0:T(8,128)(2,1)}, bf16[64,4096]{1,0:T(8,128)(2,1)S(1)}, u32[]{:S(2)}, u32[]{:S(2)}) collective-permute-start(bf16[64,4096]{1,0:T(8,128)(2,1)} %get-tuple-element.36.refs_0_), channel_id=1, source_target_pairs={{0,48},{1,17},{64,112},{65,81},{8,56},{9,25},{72,120},{73,89},{2,5... | collective-permute-start | bytes 1572872 | tf_op jit(solution)/shard_map/ppermute | solution.py:31
  139.3 10.4 %collective-permute-start.21 = (bf16[64,4096]{1,0:T(8,128)(2,1)S(1)}, bf16[64,4096]{1,0:T(8,128)(2,1)S(1)}, u32[]{:S(2)}, u32[]{:S(2)}) collective-permute-start(bf16[64,4096]{1,0:T(8,128)(2,1)S(1)} %collective-permute-done.17.refs_1_), channel_id=1, source_target_pairs={{0,16},{1,49},{64,80},{65,113},{8,24},{9,57},{72,88},{73,121},{2,1... | collective-permute-start | bytes 1572872 | tf_op jit(solution)/shard_map/ppermute | solution.py:31
  139.3 14.8 %collective-permute-start.23 = (bf16[64,4096]{1,0:T(8,128)(2,1)S(1)}, bf16[64,4096]{1,0:T(8,128)(2,1)S(1)}, u32[]{:S(2)}, u32[]{:S(2)}) collective-permute-start(bf16[64,4096]{1,0:T(8,128)(2,1)S(1)} %collective-permute-done.17.refs_1_), channel_id=1, source_target_pairs={{0,64},{1,73},{64,0},{65,9},{8,72},{9,65},{72,8},{73,1},{2,66},{3,... | collective-permute-start | bytes 1572872 | tf_op jit(solution)/shard_map/ppermute | solution.py:31
  139.8 14.4 %collective-permute-start.24 = (bf16[64,4096]{1,0:T(8,128)(2,1)S(1)}, bf16[64,4096]{1,0:T(8,128)(2,1)S(1)}, u32[]{:S(2)}, u32[]{:S(2)}) collective-permute-start(bf16[64,4096]{1,0:T(8,128)(2,1)S(1)} %collective-permute-done.18.refs_2_), channel_id=1, source_target_pairs={{0,64},{1,73},{64,0},{65,9},{8,72},{9,65},{72,8},{73,1},{2,66},{3,... | collective-permute-start | bytes 1572872 | tf_op jit(solution)/shard_map/ppermute | solution.py:31
  149.7 10.0 %collective-permute-start.22 = (bf16[64,4096]{1,0:T(8,128)(2,1)S(1)}, bf16[64,4096]{1,0:T(8,128)(2,1)S(1)}, u32[]{:S(2)}, u32[]{:S(2)}) collective-permute-start(bf16[64,4096]{1,0:T(8,128)(2,1)S(1)} %collective-permute-done.21.refs_3_), channel_id=1, source_target_pairs={{0,64},{1,73},{64,0},{65,9},{8,72},{9,65},{72,8},{73,1},{2,66},{3,... | collective-permute-start | bytes 1572872 | tf_op jit(solution)/shard_map/ppermute | solution.py:31
  150.2 24.1 %collective-permute-start.19 = (bf16[64,4096]{1,0:T(8,128)(2,1)}, bf16[64,4096]{1,0:T(8,128)(2,1)S(1)}, u32[]{:S(2)}, u32[]{:S(2)}) collective-permute-start(bf16[64,4096]{1,0:T(8,128)(2,1)} %get-tuple-element.36.refs_0_), channel_id=1, source_target_pairs={{0,64},{1,73},{64,0},{65,9},{8,72},{9,65},{72,8},{73,1},{2,66},{3,... | collective-permute-start | bytes 1572872 | tf_op jit(solution)/shard_map/ppermute | solution.py:31
  173.7 18.1 %collective-permute-start.25 = (bf16[64,4096]{1,0:T(8,128)(2,1)}, bf16[64,4096]{1,0:T(8,128)(2,1)S(1)}, u32[]{:S(2)}, u32[]{:S(2)}) collective-permute-start(bf16[64,4096]{1,0:T(8,128)(2,1)} %get-tuple-element.40), channel_id=1, source_target_pairs={{0,64},{1,73},{64,0},{65,9},{8,72},{9,65},{72,8},{73,1},{2,66},{3,... | collective-permute-start | bytes 1572872 | tf_op jit(solution)/shard_map/ppermute | solution.py:31
  188.2 22.2 %collective-permute-start.20 = (bf16[64,4096]{1,0:T(8,128)(2,1)}, bf16[64,4096]{1,0:T(8,128)(2,1)S(1)}, u32[]{:S(2)}, u32[]{:S(2)}) collective-permute-start(bf16[64,4096]{1,0:T(8,128)(2,1)} %get-tuple-element.38), channel_id=1, source_target_pairs={{0,64},{1,73},{64,0},{65,9},{8,72},{9,65},{72,8},{73,1},{2,66},{3,... | collective-permute-start | bytes 1572872 | tf_op jit(solution)/shard_map/ppermute | solution.py:31
  189.9 13.4 %collective-permute-start.27 = (bf16[64,4096]{1,0:T(8,128)(2,1)S(1)}, bf16[64,4096]{1,0:T(8,128)(2,1)S(1)}, u32[]{:S(2)}, u32[]{:S(2)}) collective-permute-start(bf16[64,4096]{1,0:T(8,128)(2,1)S(1)} %copy-done.17), channel_id=1, source_target_pairs={{0,64},{1,73},{64,0},{65,9},{8,72},{9,65},{72,8},{73,1},{2,66},{3,... | collective-permute-start | bytes 1572872 | tf_op jit(solution)/shard_map/ppermute | solution.py:31
  190.3 18.6 %collective-permute-start.29 = (bf16[64,4096]{1,0:T(8,128)(2,1)S(1)}, bf16[64,4096]{1,0:T(8,128)(2,1)S(1)}, u32[]{:S(2)}, u32[]{:S(2)}) collective-permute-start(bf16[64,4096]{1,0:T(8,128)(2,1)S(1)} %copy-done.16), channel_id=1, source_target_pairs={{0,64},{1,73},{64,0},{65,9},{8,72},{9,65},{72,8},{73,1},{2,66},{3,... | collective-permute-start | bytes 1572872 | tf_op jit(solution)/shard_map/ppermute | solution.py:31
  192.0 18.3 %collective-permute-start.26 = (bf16[64,4096]{1,0:T(8,128)(2,1)S(1)}, bf16[64,4096]{1,0:T(8,128)(2,1)S(1)}, u32[]{:S(2)}, u32[]{:S(2)}) collective-permute-start(bf16[64,4096]{1,0:T(8,128)(2,1)S(1)} %add_convert_fusion.3), channel_id=1, source_target_pairs={{0,32},{1,33},{64,96},{65,97},{8,40},{9,41},{72,104},{73,105},{2,3... | collective-permute-start | bytes 1572872 | tf_op jit(solution)/shard_map/ppermute | solution.py:31
  204.4 13.1 %collective-permute-start.28 = (bf16[64,4096]{1,0:T(8,128)(2,1)S(1)}, bf16[64,4096]{1,0:T(8,128)(2,1)S(1)}, u32[]{:S(2)}, u32[]{:S(2)}) collective-permute-start(bf16[64,4096]{1,0:T(8,128)(2,1)S(1)} %add_convert_fusion.2), channel_id=1, source_target_pairs={{0,48},{1,17},{64,112},{65,81},{8,56},{9,25},{72,120},{73,89},{2,5... | collective-permute-start | bytes 1572872 | tf_op jit(solution)/shard_map/ppermute | solution.py:31
  210.0 10.5 %collective-permute-start.30 = (bf16[64,4096]{1,0:T(8,128)(2,1)S(1)}, bf16[64,4096]{1,0:T(8,128)(2,1)S(1)}, u32[]{:S(2)}, u32[]{:S(2)}) collective-permute-start(bf16[64,4096]{1,0:T(8,128)(2,1)S(1)} %add_convert_fusion.1), channel_id=1, source_target_pairs={{0,16},{1,49},{64,80},{65,113},{8,24},{9,57},{72,88},{73,121},{2,1... | collective-permute-start | bytes 1572872 | tf_op jit(solution)/shard_map/ppermute | solution.py:31
  (25 other events, 320.0 us)
